TPU v7x, 32 devices: a 4x4x1 block of a 4x4x8 slice. The times are simulated.
32 devices in a mesh: dp: 1 (over z), col: 4 (over y), row: 8 (over x, core).
Axes of the slice: x: 4, y: 4, z: 1, core: 2. Of those that a mesh axis runs over, the one named last changes fastest.
The devices are a block of a 4x4x8 slice.
Arguments:
- x_in: bfloat16 [8, 2048, 1536], P(('dp', 'row'), None, 'col')
- ln1_scale: float32 [1536], P('col')
- ln1_shift: float32 [1536], P('col')
- w_qkv: bfloat16 [1536, 4608], P('row', 'col')
- b_qkv: float32 [16, 288], P('col')
- w_o: bfloat16 [1536, 1536], P('row', 'col')
- b_o: float32 [1536], P('col')
- ln2_scale: float32 [1536], P('col')
- ln2_shift: float32 [1536], P('col')
- w_in: bfloat16 [1536, 6144], P('row', 'col')
- b_in: float32 [6144], P('col')
- w_out: bfloat16 [6144, 1536], P('row', 'col')
- b_out: float32 [1536], P('col')
- grad_out: bfloat16 [8, 2048, 1536], P(('dp', 'row'), None, 'col')
Outputs:
- output 1: bfloat16 [8, 2048, 1536], P(('dp', 'row'), None, 'col')
- output 2: bfloat16 [8, 2048, 1536], P(('dp', 'row'), None, 'col')
- output 3: float32 [1536], P(('dp', 'col'))
- output 4: float32 [1536], P(('dp', 'col'))
- output 5: bfloat16 [1536, 4608], P(('dp', 'row'), 'col')
- output 6: float32 [16, 288], P(('dp', 'col'))
- output 7: bfloat16 [1536, 1536], P(('dp', 'row'), 'col')
- output 8: float32 [1536], P(('dp', 'col'))
- output 9: float32 [1536], P(('dp', 'col'))
- output 10: float32 [1536], P(('dp', 'col'))
- output 11: bfloat16 [1536, 6144], P(('dp', 'row'), 'col')
- output 12: float32 [6144], P(('dp', 'col'))
- output 13: bfloat16 [6144, 1536], P(('dp', 'row'), 'col')
- output 14: float32 [1536], P(('dp', 'col'))
All inputs are finite; a program needn't handle non-finite values.
Results may differ from a plain program's by a relative error of at most 0.0112138.
Values are sent between devices in bfloat16 or wider.
A program may use at most 768 MiB of HBM per device.

v0:
```python
import jax
import jax.numpy as jnp
from jax import lax
from jax.sharding import PartitionSpec as P

LN_EPS = 1e-5


def gelu_tanh(pre_act):
    return jax.nn.gelu(pre_act, approximate=True)


def attend_one(query_rows, key_rows, value_rows):
    seq_len, head_dim = query_rows.shape
    scores = lax.dot_general(query_rows, key_rows, (((1,), (1,)), ((), ())), preferred_element_type=jnp.float32)
    query_pos = lax.broadcasted_iota(jnp.int32, (seq_len, 1), 0)
    key_pos = lax.broadcasted_iota(jnp.int32, (1, seq_len), 1)
    attn_probs = jax.nn.softmax(jnp.where(key_pos <= query_pos, scores * head_dim ** -0.5, -1e30), axis=-1)
    return jnp.dot(attn_probs.astype(jnp.bfloat16), value_rows, preferred_element_type=jnp.float32).astype(jnp.bfloat16)


def attend_item(head_item):
    return attend_one(head_item[0], head_item[1], head_item[2])


def attend_item_back(item_pair):
    head_item, grad_item = item_pair
    pullback = jax.vjp(attend_one, head_item[0], head_item[1], head_item[2])[1]
    return jnp.stack(pullback(grad_item))


def layer_norm_fwd(act_blk, ln_scale, ln_shift, feat_width):
    act_f32 = act_blk.astype(jnp.float32)
    ln_stats = jnp.stack([jnp.sum(act_f32, axis=-1), jnp.sum(act_f32 * act_f32, axis=-1)], axis=-1)
    ln_stats = lax.psum(ln_stats, 'col') / feat_width
    mean_val = ln_stats[:, 0:1]
    inv_std = lax.rsqrt(ln_stats[:, 1:2] - mean_val * mean_val + LN_EPS)
    normed = (act_f32 - mean_val) * inv_std
    return (normed * ln_scale + ln_shift).astype(jnp.bfloat16), normed, inv_std


def layer_norm_bwd(grad_blk, normed, inv_std, ln_scale, feat_width):
    grad_f32 = grad_blk.astype(jnp.float32)
    grad_scale = lax.psum(jnp.sum(grad_f32 * normed, axis=0), 'row')
    grad_shift = lax.psum(jnp.sum(grad_f32, axis=0), 'row')
    grad_hat = grad_f32 * ln_scale
    grad_sums = jnp.stack([jnp.sum(grad_hat, axis=-1), jnp.sum(grad_hat * normed, axis=-1)], axis=-1)
    grad_sums = lax.psum(grad_sums, 'col') / feat_width
    grad_in = inv_std * (grad_hat - grad_sums[:, 0:1] - normed * grad_sums[:, 1:2])
    return grad_in, grad_scale, grad_shift


def gather_weight(w_blk):
    return lax.all_gather(w_blk, 'row', axis=0, tiled=True)


def gather_features(act_blk):
    return lax.all_gather(act_blk, 'col', axis=1, tiled=True)


def matmul_fwd(act_blk, w_blk):
    return jnp.dot(gather_features(act_blk), gather_weight(w_blk), preferred_element_type=jnp.float32)


def matmul_bwd(act_blk, w_blk, grad_blk):
    part_act = lax.dot_general(grad_blk, gather_weight(w_blk), (((1,), (1,)), ((), ())), preferred_element_type=jnp.float32)
    grad_act = lax.psum_scatter(part_act, 'col', scatter_dimension=1, tiled=True)
    part_w = lax.dot_general(gather_features(act_blk), grad_blk, (((0,), (0,)), ((), ())), preferred_element_type=jnp.float32)
    grad_w = lax.psum_scatter(part_w, 'row', scatter_dimension=0, tiled=True)
    return grad_act, grad_w.astype(jnp.bfloat16)


def bias_grad(grad_blk):
    return lax.psum(jnp.sum(grad_blk.astype(jnp.float32), axis=0), 'row')


def solution(mesh):
    col_size = mesh.shape['col']
    act_spec = P(('dp', 'row'), None, 'col')
    vec_spec = P('col')
    mat_spec = P('row', 'col')
    head_spec = P('col', None)
    gvec_spec = P(('dp', 'col'))
    gmat_spec = P(('dp', 'row'), 'col')
    ghead_spec = P(('dp', 'col'), None)

    def layer_block(x_blk, ln1_scale, ln1_shift, w_qkv, b_qkv, w_o, b_o, ln2_scale, ln2_shift, w_in, b_in, w_out, b_out, grad_blk):
        seq_count, seq_len, d_local = x_blk.shape
        tokens = seq_count * seq_len
        heads_local, qkv_width = b_qkv.shape
        head_dim = qkv_width // 3
        feat_width = d_local * col_size
        x_rows = x_blk.reshape(tokens, d_local)
        normed1, ln1_hat, ln1_inv = layer_norm_fwd(x_rows, ln1_scale, ln1_shift, feat_width)
        qkv_rows = (matmul_fwd(normed1, w_qkv) + b_qkv.reshape(heads_local * qkv_width)).astype(jnp.bfloat16)
        head_items = qkv_rows.reshape(seq_count, seq_len, heads_local, 3, head_dim).transpose(0, 2, 3, 1, 4).reshape(seq_count * heads_local, 3, seq_len, head_dim)
        attn_items = lax.map(attend_item, head_items)
        attn_rows = attn_items.reshape(seq_count, heads_local, seq_len, head_dim).transpose(0, 2, 1, 3).reshape(tokens, d_local)
        resid_rows = (x_rows.astype(jnp.float32) + matmul_fwd(attn_rows, w_o) + b_o).astype(jnp.bfloat16)
        normed2, ln2_hat, ln2_inv = layer_norm_fwd(resid_rows, ln2_scale, ln2_shift, feat_width)
        pre_act = matmul_fwd(normed2, w_in) + b_in
        hidden = gelu_tanh(pre_act).astype(jnp.bfloat16)
        out_rows = (resid_rows.astype(jnp.float32) + matmul_fwd(hidden, w_out) + b_out).astype(jnp.bfloat16)

        grad_rows = grad_blk.reshape(tokens, d_local)
        grad_hidden, grad_w_out = matmul_bwd(hidden, w_out, grad_rows)
        gelu_back = jax.vjp(gelu_tanh, pre_act)[1]
        grad_pre = gelu_back(grad_hidden.astype(jnp.bfloat16).astype(jnp.float32))[0]
        grad_normed2, grad_w_in = matmul_bwd(normed2, w_in, grad_pre.astype(jnp.bfloat16))
        ln2_grad, grad_ln2_scale, grad_ln2_shift = layer_norm_bwd(grad_normed2.astype(jnp.bfloat16), ln2_hat, ln2_inv, ln2_scale, feat_width)
        grad_resid = (grad_rows.astype(jnp.float32) + ln2_grad).astype(jnp.bfloat16)
        grad_attn, grad_w_o = matmul_bwd(attn_rows, w_o, grad_resid)
        grad_items = grad_attn.astype(jnp.bfloat16).reshape(seq_count, seq_len, heads_local, head_dim).transpose(0, 2, 1, 3).reshape(seq_count * heads_local, seq_len, head_dim)
        grad_heads = lax.map(attend_item_back, (head_items, grad_items))
        grad_qkv = grad_heads.reshape(seq_count, heads_local, 3, seq_len, head_dim).transpose(0, 3, 1, 2, 4).reshape(tokens, heads_local * qkv_width)
        grad_normed1, grad_w_qkv = matmul_bwd(normed1, w_qkv, grad_qkv)
        ln1_grad, grad_ln1_scale, grad_ln1_shift = layer_norm_bwd(grad_normed1.astype(jnp.bfloat16), ln1_hat, ln1_inv, ln1_scale, feat_width)
        grad_x = (grad_resid.astype(jnp.float32) + ln1_grad).astype(jnp.bfloat16)
        return (out_rows.reshape(x_blk.shape), grad_x.reshape(x_blk.shape), grad_ln1_scale, grad_ln1_shift, grad_w_qkv, bias_grad(grad_qkv).reshape(heads_local, qkv_width), grad_w_o, bias_grad(grad_resid), grad_ln2_scale, grad_ln2_shift, grad_w_in, bias_grad(grad_pre), grad_w_out, bias_grad(grad_rows))

    return jax.shard_map(layer_block, mesh=mesh,
                         in_specs=(act_spec, vec_spec, vec_spec, mat_spec, head_spec, mat_spec, vec_spec, vec_spec, vec_spec, mat_spec, vec_spec, mat_spec, vec_spec, act_spec),
                         out_specs=(act_spec, act_spec, gvec_spec, gvec_spec, gmat_spec, ghead_spec, gmat_spec, gvec_spec, gvec_spec, gvec_spec, gmat_spec, gvec_spec, gmat_spec, gvec_spec),
                         check_vma=False)
```

profile of v0, /device:TPU:96, one launch (start us, length us, event | category | flops | bytes accessed | tf_op | source)
XLA Modules:
  0.0 1750.6 jit_solution(1724202331412401182)
XLA Ops:
  10.4 18.2 %psum.84 = f32[2048,2]{0,1:T(2,128)S(1)} all-reduce(f32[2048,2]{0,1:T(2,128)S(1)} %pad_maximum_fusion), channel_id=1, replica_groups=mesh['dp'=1,'col'=4,'row'=8] {'col'}, use_global_device_ids=true, to_apply=%region_2.0 | all-reduce | flops 4096 | bytes 32768 | tf_op jit(solution)/shard_map/psum | solution.py:35
  38.8 65.3 %all-gather.9.cloned.1.call-done = bf16[2048,1536]{0,1:T(8,128)(2,1)} async-done(((bf16[2048,384]{0,1:T(8,128)(2,1)}), bf16[2048,1536]{0,1:T(8,128)(2,1)}) %all-gather.9.cloned.1.call-update) | async-done | bytes 6291472 | tf_op jit(solution)/shard_map/all_gather | solution.py:58
  104.0 12.2 add_convert_fusion
  124.4 93.2 %while.20 = (s32[]{:T(128)}, bf16[4,2048,96]{1,2,0:T(8,128)(2,1)S(1)}, bf16[4,3,2048,96]{3,2,1,0:T(8,128)(2,1)}, s32[]{:T(128)}, s32[]{:T(128)}, /*index=5*/s32[]{}, s32[]{}) while((s32[]{:T(128)}, bf16[4,2048,96]{1,2,0:T(8,128)(2,1)S(1)}, bf16[4,3,2048,96]{3,2,1,0:T(8,128)(2,1)}, s32[]{:T(128)}, s32[]{:T(128)}, /*index=5*/s32[]{}, s32[]{}) %tuple.107), condition=%wide.region_6.7_spmd, body=%wide.region_3.6_spmd.sunk | while | flops 1673719808 | bytes 119449728 | solution.py:97
  220.5 62.3 %all-gather.13.cloned.1.call-done = bf16[2048,1536]{0,1:T(8,128)(2,1)} async-done(((bf16[2048,384]{0,1:T(8,128)(2,1)}), bf16[2048,1536]{0,1:T(8,128)(2,1)}) %all-gather.13.cloned.1.call-update) | async-done | bytes 6291472 | tf_op jit(solution)/shard_map/all_gather | solution.py:58
  289.1 15.7 psum.85
  316.2 22.0 %fusion.89 = f32[2048,6144]{1,0:T(8,128)} fusion(bf16[6144,384]{1,0:T(8,128)(2,1)} %all-gather.23.cloned.1.call-done, bf16[1,2048,384]{2,1,0:T(8,128)(2,1)S(1)} %copy-done.9), kind=kOutput, calls=%fused_computation.133 | convolution fusion | flops 9663676416 | bytes 56623104 | tf_op jit(solution)/shard_map/dot_general | solution.py:66
  349.2 65.5 %all-gather.17.cloned.1.call-done = bf16[2048,1536]{0,1:T(8,128)(2,1)} async-done(((bf16[2048,384]{0,1:T(8,128)(2,1)}), bf16[2048,1536]{0,1:T(8,128)(2,1)}) %all-gather.17.cloned.1.call-update) | async-done | bytes 6291472 | tf_op jit(solution)/shard_map/all_gather | solution.py:58
  414.6 418.4 %reduce-scatter.9.cloned.1.call-done = f32[2048,1536]{1,0:T(8,128)} async-done(((f32[2048,6144]{1,0:T(8,128)}), f32[2048,1536]{1,0:T(8,128)}) %reduce-scatter.9.cloned.1.call-update) | async-done | bytes 12582928 | tf_op jit(solution)/shard_map/reduce_scatter | solution.py:67
  833.1 28.0 %fusion.95 = (f32[1536]{0:T(1024)}, bf16[2048,1536]{1,0:T(8,128)(2,1)}, bf16[2048,1536]{1,0:T(8,128)(2,1)}) fusion(f32[1536]{0:T(1024)S(1)} %copy-done.30, f32[2048,1536]{1,0:T(8,128)} %reduce-scatter.9.cloned.1.call-done, bf16[2048,1536]{0,1:T(8,128)(2,1)} %all-gather.17.cloned.1.call-done, bf16[1536,1536]{1,0:T(8,128)(2,1)} %all-gather.19.cloned.1.call-done), kind=kOutput, calls=%fused_computation.149 | convolution fusion | flops 9745463296 | bytes 36188160 | tf_op jit(solution)/shard_map/dot_general | solution.py:62
  861.0 16.0 fusion.83
  879.5 109.4 %reduce-scatter.11.cloned.1.call-done = f32[2048,384]{0,1:T(8,128)} async-done(((f32[2048,1536]{0,1:T(8,128)}), f32[2048,384]{0,1:T(8,128)}) %reduce-scatter.11.cloned.1.call-update) | async-done | bytes 3145744 | tf_op jit(solution)/shard_map/reduce_scatter | solution.py:67
  993.8 15.0 psum.86
  1021.7 15.9 fusion.81
  1045.7 166.5 %all-gather.21.cloned.1.call-done = bf16[2048,6144]{1,0:T(8,128)(2,1)} async-done(((bf16[2048,1536]{1,0:T(8,128)(2,1)}), bf16[2048,6144]{1,0:T(8,128)(2,1)}) %all-gather.21.cloned.1.call-update) | async-done | bytes 25165840 | tf_op jit(solution)/shard_map/all_gather | solution.py:58
  1212.2 20.2 %fusion.87 = f32[6144,384]{1,0:T(8,128)} fusion(bf16[2048,6144]{1,0:T(8,128)(2,1)} %all-gather.21.cloned.1.call-done, bf16[1,2048,384]{2,1,0:T(8,128)(2,1)S(1)} %copy-done.10), kind=kOutput, calls=%fused_computation.131 | convolution fusion | flops 9663676416 | bytes 36175872 | tf_op jit(solution)/shard_map/dot_general | solution.py:68
  1232.5 94.8 %reduce-scatter.13.cloned.1.call-done = f32[2048,384]{1,0:T(8,128)} async-done(((f32[2048,1536]{1,0:T(8,128)}), f32[2048,384]{1,0:T(8,128)}) %reduce-scatter.13.cloned.1.call-update) | async-done | bytes 3145744 | tf_op jit(solution)/shard_map/reduce_scatter | solution.py:67
  1330.2 191.7 %while.21 = (s32[]{:T(128)}, bf16[4,3,2048,96]{2,3,1,0:T(8,128)(2,1)}, bf16[4,2048,96]{1,2,0:T(8,128)(2,1)S(1)}, bf16[4,3,2048,96]{3,2,1,0:T(8,128)(2,1)}, s32[]{:T(128)}, /*index=5*/s32[]{:T(128)}, s32[]{}, s32[]{}) while((s32[]{:T(128)}, bf16[4,3,2048,96]{2,3,1,0:T(8,128)(2,1)}, bf16[4,2048,96]{1,2,0:T(8,128)(2,1)S(1)}, ...), condition=%wide.region_20.21_spmd, body=%wide.region_16.0_spmd.sunk | while | flops 4177068032 | bytes 250343168 | solution.py:114
  1340.4 11.9 fusion.153
  1352.3 12.7 fusion.154
  1388.1 11.9 fusion.153
  1400.1 12.7 fusion.154
  1435.9 11.9 fusion.153
  1447.9 12.7 fusion.154
  1483.7 12.0 fusion.153
  1495.7 12.7 fusion.154
  1521.9 13.6 fusion.103
  1537.5 13.1 fusion.105
  1554.6 15.0 fusion.85
  1581.0 112.0 %reduce-scatter.15.cloned.1.call-done = f32[2048,384]{0,1:T(8,128)} async-done(((f32[2048,1536]{0,1:T(8,128)}), f32[2048,384]{0,1:T(8,128)}) %reduce-scatter.15.cloned.1.call-update) | async-done | bytes 3145744 | tf_op jit(solution)/shard_map/reduce_scatter | solution.py:67
  1697.4 15.4 psum.87
  1719.4 24.3 %all-reduce = (f32[384]{0:T(512)}, f32[384]{0:T(512)}, f32[4,288]{1,0:T(4,128)}, f32[384]{0:T(512)}, f32[384]{0:T(512)}, /*index=5*/f32[384]{0:T(512)}, f32[1536]{0:T(1024)}, f32[384]{0:T(512)}) all-reduce(f32[384]{0:T(512)S(1)} %get-tuple-element.89, ...), channel_id=1, replica_groups=mesh['dp'=1,'col'=4,'row'=8] {'row'}, use_global_device_ids=true, to_apply=%region_26.27 | all-reduce | flops 4992 | bytes 39936 | tf_op jit(solution)/shard_map/psum | solution.py:44
  (237 shorter events, 297.6 us)
Async XLA Ops:
  7.2 31.6 %all-gather.11.cloned.1.call-start = ((), (), s32[]{:S(2)}) async-start(), calls=%async_computation.9 | async-start | bytes 3981312 | tf_op jit(solution)/shard_map/all_gather | solution.py:54
  8.0 96.0 %all-gather.9.cloned.1.call-start = ((), (), s32[]{:S(2)}) async-start(), calls=%async_computation.8 | async-start | bytes 7864320 | tf_op jit(solution)/shard_map/all_gather | solution.py:58
  9.8 106.5 %copy-start.2 = (bf16[1,2048,384]{1,2,0:T(8,128)(2,1)}, bf16[1,2048,384]{1,2,0:T(8,128)(2,1)S(1)}, u32[]{:S(2)}) copy-start(bf16[1,2048,384]{1,2,0:T(8,128)(2,1)S(1)} %copy.37) | copy-start | bytes 4718596
  31.2 189.3 %all-gather.15.cloned.1.call-start = ((), (), s32[]{:S(2)}) async-start(), calls=%async_computation.11 | async-start | bytes 1327104 | tf_op jit(solution)/shard_map/all_gather | solution.py:54
  32.0 250.8 %all-gather.13.cloned.1.call-start = ((), (), s32[]{:S(2)}) async-start(), calls=%async_computation.10 | async-start | bytes 7864320 | tf_op jit(solution)/shard_map/all_gather | solution.py:58
  124.4 158.4 %copy-start.3 = (bf16[1,2048,384]{1,2,0:T(8,128)(2,1)S(1)}, bf16[1,2048,384]{1,2,0:T(8,128)(2,1)}, u32[]{:S(2)}) copy-start(bf16[1,2048,384]{1,2,0:T(8,128)(2,1)} %copy-done.2) | copy-start | bytes 4718596
  124.4 158.4 %copy-start.31 = (f32[384]{0:T(512)S(1)}, f32[384]{0:T(512)}, u32[]{:S(2)}) copy-start(f32[384]{0:T(512)} %param.24) | copy-start | bytes 4612
  218.8 97.4 %all-gather.23.cloned.1.call-start = ((), (), s32[]{:S(2)}) async-start(), calls=%async_computation.15 | async-start | bytes 5308416 | tf_op jit(solution)/shard_map/all_gather | solution.py:54
  219.5 129.7 %all-gather.19.cloned.1.call-start = ((), (), s32[]{:S(2)}) async-start(), calls=%async_computation.13 | async-start | bytes 5308416 | tf_op jit(solution)/shard_map/all_gather | solution.py:54
  220.1 84.7 %copy-start.17 = (f32[384]{0:T(512)S(1)}, f32[384]{0:T(512)}, u32[]{:S(2)}) copy-start(f32[384]{0:T(512)} %param.25) | copy-start | bytes 4612
  220.1 84.7 %copy-start.27 = (f32[384]{0:T(512)S(1)}, f32[384]{0:T(512)}, u32[]{:S(2)}) copy-start(f32[384]{0:T(512)} %param.26) | copy-start | bytes 4612
  220.1 194.5 %all-gather.17.cloned.1.call-start = ((), (), s32[]{:S(2)}) async-start(), calls=%async_computation.12 | async-start | bytes 7864320 | tf_op jit(solution)/shard_map/all_gather | solution.py:58
  289.0 719.8 %copy-start.7 = (bf16[2048,384]{0,1:T(8,128)(2,1)}, bf16[2048,384]{0,1:T(8,128)(2,1)S(1)}, u32[]{:S(2)}) copy-start(bf16[2048,384]{0,1:T(8,128)(2,1)S(1)} %get-tuple-element.141) | copy-start | bytes 4718596
  289.1 27.2 %copy-start.9 = (bf16[1,2048,384]{2,1,0:T(8,128)(2,1)S(1)}, bf16[1,2048,384]{2,1,0:T(8,128)(2,1)}, u32[]{:S(2)}) copy-start(bf16[1,2048,384]{2,1,0:T(8,128)(2,1)} %param.31) | copy-start | bytes 4718596
  306.6 526.4 %reduce-scatter.9.cloned.1.call-start = ((), (), s32[]{:S(2)}) async-start(), calls=%async_computation.16 | async-start | bytes 62914560 | tf_op jit(solution)/shard_map/reduce_scatter | solution.py:67
  338.3 494.8 %copy-start.30 = (f32[1536]{0:T(1024)S(1)}, f32[1536]{0:T(1024)}, u32[]{:S(2)}) copy-start(f32[1536]{0:T(1024)} %param.28) | copy-start | bytes 18436
  338.3 650.6 %reduce-scatter.11.cloned.1.call-start = ((), (), s32[]{:S(2)}) async-start(), calls=%async_computation.17 | async-start | bytes 15728640 | tf_op jit(solution)/shard_map/reduce_scatter | solution.py:67
  833.1 28.0 %copy-start.28 = (bf16[1536,1536]{1,0:T(8,128)(2,1)S(1)}, bf16[1536,1536]{1,0:T(8,128)(2,1)}, u32[]{:S(2)}) copy-start(bf16[1536,1536]{1,0:T(8,128)(2,1)} %all-gather.19.cloned.1.call-done) | copy-start | bytes 14155780
  877.1 335.1 %all-gather.21.cloned.1.call-start = ((), (), s32[]{:S(2)}) async-start(), calls=%async_computation.14 | async-start | bytes 31457280 | tf_op jit(solution)/shard_map/all_gather | solution.py:58
  877.7 449.7 %reduce-scatter.13.cloned.1.call-start = ((), (), s32[]{:S(2)}) async-start(), calls=%async_computation.18 | async-start | bytes 15728640 | tf_op jit(solution)/shard_map/reduce_scatter | solution.py:67
  1013.3 24.5 %copy-start.5 = (bf16[2048,384]{0,1:T(8,128)(2,1)}, bf16[2048,384]{0,1:T(8,128)(2,1)S(1)}, u32[]{:S(2)}) copy-start(bf16[2048,384]{0,1:T(8,128)(2,1)S(1)} %get-tuple-element.122) | copy-start | bytes 4718596
  1021.6 529.0 %reduce-scatter.21.cloned.1.call-start = ((), (), s32[]{:S(2)}) async-start(), calls=%async_computation.22 | async-start | bytes 10616832 | tf_op jit(solution)/shard_map/reduce_scatter | solution.py:69
  1037.7 174.5 %copy-start.10 = (bf16[1,2048,384]{2,1,0:T(8,128)(2,1)S(1)}, bf16[1,2048,384]{2,1,0:T(8,128)(2,1)}, u32[]{:S(2)}) copy-start(bf16[1,2048,384]{2,1,0:T(8,128)(2,1)} %param.31) | copy-start | bytes 4718596
  1037.7 515.2 %reduce-scatter.19.cloned.1.call-start = ((), (), s32[]{:S(2)}) async-start(), calls=%async_computation.21 | async-start | bytes 2654208 | tf_op jit(solution)/shard_map/reduce_scatter | solution.py:69
  1045.6 528.8 %reduce-scatter.23.cloned.1.call-start = ((), (), s32[]{:S(2)}) async-start(), calls=%async_computation.23 | async-start | bytes 10616832 | tf_op jit(solution)/shard_map/reduce_scatter | solution.py:69
  1232.5 346.6 %reduce-scatter.17.cloned.1.call-start = ((), (), s32[]{:S(2)}) async-start(), calls=%async_computation.20 | async-start | bytes 7962624 | tf_op jit(solution)/shard_map/reduce_scatter | solution.py:69
  1535.6 157.5 %reduce-scatter.15.cloned.1.call-start = ((), (), s32[]{:S(2)}) async-start(), calls=%async_computation.19 | async-start | bytes 15728640 | tf_op jit(solution)/shard_map/reduce_scatter | solution.py:67
  1569.6 123.5 %copy-start.4 = (bf16[1,2048,384]{1,2,0:T(8,128)(2,1)S(1)}, bf16[1,2048,384]{1,2,0:T(8,128)(2,1)}, u32[]{:S(2)}) copy-start(bf16[1,2048,384]{1,2,0:T(8,128)(2,1)} %copy-done.2) | copy-start | bytes 4718596
  1569.6 123.5 %copy-start.14 = (f32[2048,1]{0,1:T(1,128)S(1)}, f32[2048,1]{0,1:T(1,128)}, u32[]{:S(2)}) copy-start(f32[2048,1]{0,1:T(1,128)} %copy-done.13) | copy-start | bytes 24580
  1569.6 123.5 %copy-start.16 = (f32[2048,1]{0,1:T(1,128)S(1)}, f32[2048,1]{0,1:T(1,128)}, u32[]{:S(2)}) copy-start(f32[2048,1]{0,1:T(1,128)} %copy-done.15) | copy-start | bytes 24580
  1569.6 123.5 %copy-start.19 = (f32[384]{0:T(512)S(1)}, f32[384]{0:T(512)}, u32[]{:S(2)}) copy-start(f32[384]{0:T(512)} %param.19) | copy-start | bytes 4612
  1574.3 138.5 %copy-start.6 = (bf16[2048,384]{0,1:T(8,128)(2,1)S(1)}, bf16[2048,384]{0,1:T(8,128)(2,1)}, u32[]{:S(2)}) copy-start(bf16[2048,384]{0,1:T(8,128)(2,1)} %copy-done.5) | copy-start | bytes 4718596
  (39 other events, 421.7 us)
Sparse Core Ops, SparseCore 0:
  9.6 29.0 all-gather.10
  40.9 63.0 all-gather.8
  105.6 21.3 all-gather.14
  219.0 63.7 all-gather.12
  284.2 31.9 all-gather.22
  317.7 31.4 all-gather.18
  351.3 63.2 all-gather.16
  417.0 416.0 reduce-scatter.8
  877.2 111.6 reduce-scatter.10
  990.3 221.7 all-gather.20
  1214.6 112.7 reduce-scatter.12
  1329.6 54.5 reduce-scatter.20
  1386.5 31.5 reduce-scatter.18
  1420.2 53.7 reduce-scatter.22
  1535.7 43.3 reduce-scatter.16
  1581.3 111.7 reduce-scatter.14
where the time goes:
time: 1750 us
  waiting for transfers between devices  1130 us (65%)
  matrix products  343 us (20%)
  other arithmetic  128 us (7%)
  blocking collectives  88.6 us (5%)
  local copies, waits for them, and re-layouts  47.4 us (3%)
    reduce_scatter x4, waiting for transfers between devices, matmul_bwd(): lax.psum_scatter(part_act, 'col', scatter_dimension=1, tiled=True)  735 us
    all_gather x4, waiting for transfers between devices, gather_features(): return lax.all_gather(act_blk, 'col', axis=1, tiled=True)  360 us
    dot_general x12, matrix products, attend_one(): jnp.dot(attn_probs.astype(jnp.bfloat16), value_rows, preferred_element_ty...  105 us
    dot_general x4, matrix products, matmul_fwd(): jnp.dot(gather_features(act_blk), gather_weight(w_blk), preferred_element...  61.4 us
    dot_general x16, matrix products, attend_one(): lax.dot_general(query_rows, key_rows, (((1,), (1,)), ((), ())), preferred...  59.7 us
    dot_general x4, matrix products, matmul_bwd(): lax.dot_general(grad_blk, gather_weight(w_blk), (((1,), (1,)), ((), ())),...  59.4 us
    dot_general x4, matrix products, matmul_bwd(): lax.dot_general(gather_features(act_blk), grad_blk, (((0,), (0,)), ((), (...  57.5 us
    mul x4, other arithmetic, attend_one(): scores * head_dim ** (-0.5)  50.7 us
  transfers between devices with their start and end apart: 16, of which 12 were waited for; matrix products, arithmetic and copies ran while one was open for 25% of the time, Pallas kernels for 0%

commit v1 on v0

v1 whole, which is shorter than its diff:
```python
import functools

import jax
import jax.numpy as jnp
from jax import lax
from jax.experimental import pallas as pl
from jax.experimental.pallas import tpu as pltpu
from jax.sharding import PartitionSpec as P

LN_EPS = 1e-5
LANES = 128
Q_BLOCK = 256
BF16 = jnp.bfloat16
F32 = jnp.float32


def gelu_tanh(pre_act):
    return jax.nn.gelu(pre_act, approximate=True)


def dot(lhs, rhs):
    return jnp.dot(lhs, rhs, preferred_element_type=F32)


def dot_tr(lhs, rhs):
    return lax.dot_general(lhs, rhs, (((1,), (1,)), ((), ())), preferred_element_type=F32)


def dot_tl(lhs, rhs):
    return lax.dot_general(lhs, rhs, (((0,), (0,)), ((), ())), preferred_element_type=F32)


def attn_fwd_kernel(scale, blk, q_ref, k_ref, v_ref, o_ref, m_ref, r_ref):
    seq_len = q_ref.shape[0]
    vals_t = v_ref[...].astype(F32).T.astype(BF16)
    key_pos = lax.broadcasted_iota(jnp.int32, (blk, blk), 0)
    query_pos = lax.broadcasted_iota(jnp.int32, (blk, blk), 1)
    keep = key_pos <= query_pos
    for start in range(0, seq_len, blk):
        rows = pl.ds(start, blk)
        query = q_ref[rows, :]
        diag = jnp.where(keep, dot_tr(k_ref[rows, :], query) * scale, -1e30)
        top = jnp.max(diag, axis=0, keepdims=True)
        if start:
            past = dot_tr(k_ref[pl.ds(0, start), :], query) * scale
            top = jnp.maximum(top, jnp.max(past, axis=0, keepdims=True))
            past = jnp.exp(past - top)
        diag = jnp.exp(diag - top)
        total = jnp.sum(diag, axis=0, keepdims=True)
        if start:
            total = total + jnp.sum(past, axis=0, keepdims=True)
        recip = 1.0 / total
        out_t = dot(vals_t[:, start:start + blk], (diag * recip).astype(BF16))
        if start:
            out_t = out_t + dot(vals_t[:, :start], (past * recip).astype(BF16))
        o_ref[rows, :] = out_t.T.astype(BF16)
        m_ref[0, :, rows] = top
        r_ref[0, :, rows] = recip


def attn_bwd_kernel(scale, blk, q_ref, k_ref, v_ref, do_ref, m_ref, r_ref, dq_ref, dk_ref, dv_ref, dk_acc, dv_acc):
    seq_len = q_ref.shape[0]
    keys_t = k_ref[...].astype(F32).T.astype(BF16)
    key_pos = lax.broadcasted_iota(jnp.int32, (blk, blk), 0)
    query_pos = lax.broadcasted_iota(jnp.int32, (blk, blk), 1)
    keep = key_pos <= query_pos
    dk_acc[...] = jnp.zeros_like(dk_acc)
    dv_acc[...] = jnp.zeros_like(dv_acc)
    for start in range(0, seq_len, blk):
        rows = pl.ds(start, blk)
        query, grad = q_ref[rows, :], do_ref[rows, :]
        top, recip = m_ref[0, :, rows], r_ref[0, :, rows]

        def probs_of(span, masked):
            scores = dot_tr(k_ref[span, :], query) * scale
            if masked:
                scores = jnp.where(keep, scores, -1e30)
            probs = jnp.exp(scores - top) * recip
            dv_acc[span, :] += dot(probs.astype(BF16), grad)
            gprobs = dot_tr(v_ref[span, :], grad)
            return probs, gprobs, jnp.sum(probs * gprobs, axis=0, keepdims=True)

        spans = [(rows, True, start, start + blk)]
        if start:
            spans.append((pl.ds(0, start), False, 0, start))
        parts = [probs_of(span, masked) for span, masked, _, _ in spans]
        delta = parts[0][2]
        if start:
            delta = delta + parts[1][2]
        dq_t = None
        for (span, _, lo, hi), (probs, gprobs, _) in zip(spans, parts):
            gscores = (probs * (gprobs - delta) * scale).astype(BF16)
            dk_acc[span, :] += dot(gscores, query)
            term = dot(keys_t[:, lo:hi], gscores)
            dq_t = term if dq_t is None else dq_t + term
        dq_ref[rows, :] = dq_t.T.astype(BF16)
    dk_ref[...] = dk_acc[...].astype(BF16)
    dv_ref[...] = dv_acc[...].astype(BF16)


def attn_specs(seq_len, part):
    return pl.BlockSpec((seq_len, LANES), lambda i, h: (i, 3 * h + part))


def attention_fwd(qkv_pad, seq_count, heads, head_dim):
    seq_len = qkv_pad.shape[0] // seq_count
    items = seq_count * heads
    head_spec = pl.BlockSpec((seq_len, LANES), lambda i, h: (i, h))
    stat_spec = pl.BlockSpec((1, 1, seq_len), lambda i, h: (i * heads + h, 0, 0))
    flops = items * 4 * seq_len * seq_len * LANES // 2
    return pl.pallas_call(
        functools.partial(attn_fwd_kernel, head_dim ** -0.5, min(Q_BLOCK, seq_len)),
        grid=(seq_count, heads),
        in_specs=[attn_specs(seq_len, part) for part in range(3)],
        out_specs=[head_spec, stat_spec, stat_spec],
        out_shape=[jax.ShapeDtypeStruct((qkv_pad.shape[0], heads * LANES), BF16)] + [jax.ShapeDtypeStruct((items, 1, seq_len), F32)] * 2,
        cost_estimate=pl.CostEstimate(flops=8 * flops, bytes_accessed=qkv_pad.size * 3, transcendentals=0),
        compiler_params=pltpu.CompilerParams(vmem_limit_bytes=48 << 20),
        name="attn_fwd",
    )(qkv_pad, qkv_pad, qkv_pad)


def attention_bwd(qkv_pad, grad_pad, tops, recips, seq_count, heads, head_dim):
    seq_len = qkv_pad.shape[0] // seq_count
    items = seq_count * heads
    head_spec = pl.BlockSpec((seq_len, LANES), lambda i, h: (i, h))
    stat_spec = pl.BlockSpec((1, 1, seq_len), lambda i, h: (i * heads + h, 0, 0))
    flops = items * 10 * seq_len * seq_len * LANES // 2
    return pl.pallas_call(
        functools.partial(attn_bwd_kernel, head_dim ** -0.5, min(Q_BLOCK, seq_len)),
        grid=(seq_count, heads),
        in_specs=[attn_specs(seq_len, part) for part in range(3)] + [head_spec, stat_spec, stat_spec],
        out_specs=[head_spec] * 3,
        out_shape=[jax.ShapeDtypeStruct((qkv_pad.shape[0], heads * LANES), BF16)] * 3,
        scratch_shapes=[pltpu.VMEM((seq_len, LANES), F32)] * 2,
        cost_estimate=pl.CostEstimate(flops=8 * flops, bytes_accessed=qkv_pad.size * 4, transcendentals=0),
        compiler_params=pltpu.CompilerParams(vmem_limit_bytes=48 << 20),
        name="attn_bwd",
    )(qkv_pad, qkv_pad, qkv_pad, grad_pad, tops, recips)


def pad_heads(arr, heads, head_dim):
    lead = arr.shape[:-1]
    arr = arr.reshape(lead + (heads, head_dim))
    arr = jnp.pad(arr, [(0, 0)] * (len(lead) + 1) + [(0, LANES - head_dim)])
    return arr.reshape(lead + (heads * LANES,))


def unpad_heads(arr, heads, head_dim):
    lead = arr.shape[:-1]
    return arr.reshape(lead + (heads, LANES))[..., :head_dim].reshape(lead + (heads * head_dim,))


def norm_rows(act_f32):
    mean_val = jnp.mean(act_f32, axis=-1, keepdims=True)
    variance = jnp.mean(act_f32 * act_f32, axis=-1, keepdims=True) - mean_val * mean_val
    inv_std = lax.rsqrt(variance + LN_EPS)
    return (act_f32 - mean_val) * inv_std, inv_std


def layer_norm(act_in, ln_scale, ln_shift):
    return (norm_rows(act_in.astype(F32))[0] * ln_scale + ln_shift).astype(BF16)


def layer_norm_bwd(grad_bf16, act_in, ln_scale):
    grad_f32 = grad_bf16.astype(F32)
    normed, inv_std = norm_rows(act_in.astype(F32))
    grad_hat = grad_f32 * ln_scale
    mean_a = jnp.mean(grad_hat, axis=-1, keepdims=True)
    mean_b = jnp.mean(grad_hat * normed, axis=-1, keepdims=True)
    grad_in = inv_std * (grad_hat - mean_a - normed * mean_b)
    return grad_in, jnp.sum(grad_f32 * normed, axis=0), jnp.sum(grad_f32, axis=0)


def ring_gather(blk, size, axis):
    me = lax.axis_index('col')
    width = blk.shape[axis]
    up = [(i, (i + 1) % size) for i in range(size)]
    down = [(i, (i - 1) % size) for i in range(size)]
    half = blk.shape[0] // 2
    whole_shape = list(blk.shape)
    whole_shape[axis] = width * size

    def place(whole, part, owner, row_off):
        offs = [0] * blk.ndim
        offs[0] = row_off
        offs[axis] = offs[axis] + lax.rem(owner + 2 * size, size) * width
        return lax.dynamic_update_slice(whole, part, tuple(offs))

    whole = place(jnp.zeros(tuple(whole_shape), blk.dtype), blk, me, 0)
    from_low = lax.ppermute(blk, 'col', up)
    from_high = lax.ppermute(blk, 'col', down)
    far_a = lax.ppermute(from_low[:half], 'col', up)
    far_b = lax.ppermute(from_high[half:], 'col', down)
    whole = place(whole, from_low, me - 1, 0)
    whole = place(whole, from_high, me + 1, 0)
    whole = place(whole, far_a, me + 2, 0)
    return place(whole, far_b, me + 2, half)


def tie(value, *others):
    return lax.optimization_barrier((value, *others))


def ring_scatter(part, size, axis, between=None):
    me = lax.axis_index('col')
    width = part.shape[axis] // size
    up = [(i, (i + 1) % size) for i in range(size)]
    down = [(i, (i - 1) % size) for i in range(size)]

    def block(owner):
        return lax.dynamic_slice_in_dim(part, lax.rem(owner + size, size) * width, width, axis)

    far, high, low, own = block(me + 2), block(me + 1), block(me - 1), block(me)
    half = own.shape[0] // 2
    from_low = lax.ppermute(far[:half], 'col', up)
    from_high = lax.ppermute(far[half:], 'col', down)
    if between is not None:
        from_low, from_high = between(from_low, from_high)
    got_a = lax.ppermute(jnp.concatenate([high[:half] + from_low, high[half:]], axis=0), 'col', up)
    got_b = lax.ppermute(jnp.concatenate([low[:half], low[half:] + from_high], axis=0), 'col', down)
    return own + got_a + got_b


def exchange(arr, size, split_axis, join_axis):
    me = lax.axis_index('col')
    width = arr.shape[split_axis] // size
    shape = list(arr.shape)
    shape[split_axis] = width
    join = shape[join_axis]
    shape[join_axis] = join * size
    whole = jnp.zeros(tuple(shape), arr.dtype)
    for shift in range(size):
        target = lax.rem(me + shift, size)
        part = lax.dynamic_slice_in_dim(arr, target * width, width, split_axis)
        if shift:
            part = lax.ppermute(part, 'col', [(i, (i + shift) % size) for i in range(size)])
        source = lax.rem(me + size - shift, size)
        whole = lax.dynamic_update_slice_in_dim(whole, part, source * join, join_axis)
    return whole


def solution(mesh):
    cols = mesh.shape['col']
    rows = mesh.shape['row']
    per = rows // cols
    assert cols == 4 and rows == cols * per
    act_spec = P(('dp', 'row'), None, 'col')
    vec_spec = P('col')
    mat_spec = P('row', 'col')
    head_spec = P('col', None)
    gvec_spec = P(('dp', 'col'))
    gmat_spec = P(('dp', 'row'), 'col')
    ghead_spec = P(('dp', 'col'), None)
    flip = [(b * rows + a * per + k, a * rows + b * per + k) for a in range(cols) for k in range(per) for b in range(cols)]

    def gather_rows(w_blk):
        return lax.all_gather(w_blk, 'row', axis=0, tiled=True)

    def gather_vec(vec):
        return lax.all_gather(vec, 'col', axis=0, tiled=True)

    def scatter_rows(part):
        return lax.psum_scatter(part, 'row', scatter_dimension=0, tiled=True)

    def row_split_weight(w_blk):
        depth, width = w_blk.shape
        moved = lax.ppermute(w_blk, ('col', 'row'), flip)
        stack = gather_rows(moved).reshape(cols, per, depth, width)
        return stack.transpose(1, 2, 0, 3).reshape(per * depth, cols * width)

    def row_split_part(lhs, rhs):
        width = rhs.shape[1] // cols
        depth = lhs.shape[1] // per
        part = jnp.concatenate([dot_tl(lhs, rhs[:, j * width:(j + 1) * width]) for j in range(cols)], axis=0)
        return part.reshape(rows * depth, width)

    def to_owner(block):
        return lax.ppermute(block.astype(BF16), ('col', 'row'), flip)

    def layer_block(x_blk, ln1_scale, ln1_shift, w_qkv, b_qkv, w_o, b_o, ln2_scale, ln2_shift, w_in, b_in, w_out, b_out, grad_blk):
        seq_count, seq_len, d_local = x_blk.shape
        tokens = seq_count * seq_len
        tok_local = tokens // cols
        heads, qkv_width = b_qkv.shape
        head_dim = qkv_width // 3
        me = lax.axis_index('col')
        x_loc = x_blk.reshape(tokens, d_local)
        g_loc = grad_blk.reshape(tokens, d_local)

        def own_tokens(arr):
            return lax.dynamic_slice_in_dim(arr, me * tok_local, tok_local, 0)

        def own_feats(arr):
            return lax.dynamic_slice_in_dim(arr, me * d_local, d_local, arr.ndim - 1)

        vecs = gather_vec(jnp.stack([ln1_scale, ln1_shift, ln2_scale, ln2_shift, b_o], axis=1))
        scale1, shift1, scale2, shift2, bias_o = [vecs[:, i] for i in range(5)]

        x_full = ring_gather(x_loc, cols, 1)
        w_qkv_full = gather_rows(w_qkv)
        w_out_blk, w_o_blk, w_in_blk, g_blk, x_full = lax.optimization_barrier((w_out, w_o, w_in, g_loc, x_full))
        w_o_full = ring_gather(gather_rows(w_o_blk), cols, 1)
        w_out_rows = row_split_weight(w_out_blk)
        w_in_full = gather_rows(w_in_blk)
        g_full = ring_gather(g_blk, cols, 1)

        normed1 = layer_norm(x_full, scale1, shift1)
        w_qkv_pad = pad_heads(w_qkv_full, 3 * heads, head_dim)
        b_qkv_pad = pad_heads(b_qkv.reshape(heads * qkv_width), 3 * heads, head_dim)
        qkv_pad = (dot(normed1, w_qkv_pad) + b_qkv_pad).astype(BF16)
        o_pad, tops, recips = attention_fwd(qkv_pad, seq_count, heads, head_dim)
        o_loc = unpad_heads(o_pad, heads, head_dim)
        o_tok = exchange(o_loc, cols, 0, 1)
        r1_tok = (own_tokens(x_full).astype(F32) + dot(o_tok, w_o_full) + bias_o).astype(BF16)
        grad_hidden = dot_tr(g_full, w_out_rows).astype(BF16)
        r1_full = ring_gather(r1_tok, cols, 0)
        normed2 = layer_norm(r1_full, scale2, shift2)
        pre_act = dot(normed2, w_in_full) + b_in
        hidden, gelu_back = jax.vjp(gelu_tanh, pre_act)
        hidden = hidden.astype(BF16)
        grad_pre = gelu_back(grad_hidden.astype(F32))[0]
        grad_pre_bf = grad_pre.astype(BF16)

        gh2 = ring_scatter(dot_tr(grad_pre_bf, w_in_full), cols, 0).astype(BF16)
        gh2, part_w_out, out_part = tie(gh2, row_split_part(hidden, g_full), dot(hidden, w_out_rows))
        ln2_grad, ln2_gscale, ln2_gshift = layer_norm_bwd(gh2, r1_tok, scale2)
        gr1_tok = (own_tokens(g_full).astype(F32) + ln2_grad).astype(BF16)
        gr1_full = ring_gather(gr1_tok, cols, 0)
        gr1_full, part_w_in, out_part = tie(gr1_full, dot_tl(normed2, grad_pre_bf), out_part)
        w_o_pad = pad_heads(lax.dynamic_slice_in_dim(w_o_full, me * d_local, d_local, 0).T, heads, head_dim)
        grad_o_pad = dot(gr1_full, w_o_pad).astype(BF16)
        grad_o_pad, sum_w_out = tie(grad_o_pad, scatter_rows(part_w_out))
        dq, dk, dv = attention_bwd(qkv_pad, grad_o_pad, tops, recips, seq_count, heads, head_dim)
        grads = [a.reshape(tokens, heads, LANES)[..., :head_dim] for a in (dq, dk, dv)]
        grad_qkv = jnp.stack(grads, axis=2).reshape(tokens, heads * qkv_width)

        def under_attention(from_low, from_high):
            nonlocal grad_qkv
            grad_qkv, from_low, from_high = tie(grad_qkv, from_low, from_high)
            return from_low, from_high

        out_sum = ring_scatter(out_part, cols, 1, under_attention)
        out_rows = (own_feats(r1_full).astype(F32) + out_sum + b_out).astype(BF16)
        gh1 = ring_scatter(dot_tr(grad_qkv, w_qkv_full), cols, 0).astype(BF16)
        gh1, part_w_o, part_w_qkv, sum_w_in = tie(gh1, row_split_part(o_loc, gr1_full), dot_tl(normed1, grad_qkv), scatter_rows(part_w_in))
        ln1_grad, ln1_gscale, ln1_gshift = layer_norm_bwd(gh1, own_tokens(x_full), scale1)
        gx_tok = (gr1_tok.astype(F32) + ln1_grad).astype(BF16)
        grad_x = exchange(gx_tok, cols, 1, 0)

        grad_w_out = to_owner(sum_w_out)
        grad_w_in = sum_w_in.astype(BF16)
        grad_w_o = to_owner(scatter_rows(part_w_o))
        grad_w_qkv = scatter_rows(part_w_qkv).astype(BF16)

        def tok_sum(arr):
            return jnp.sum(arr.astype(F32), axis=0)

        early = lax.psum(jnp.concatenate([tok_sum(grad_pre), tok_sum(g_loc), tok_sum(own_feats(gr1_full)), tok_sum(grad_qkv)]), 'row')
        ff_local = b_in.shape[0]
        gb_in, gb_out, gb_o, gb_qkv = jnp.split(early, [ff_local, ff_local + d_local, ff_local + 2 * d_local])
        late = lax.psum(jnp.stack([ln1_gscale, ln1_gshift, ln2_gscale, ln2_gshift]), ('col', 'row'))
        g_ln = own_feats(late)
        return (out_rows.reshape(x_blk.shape), grad_x.reshape(x_blk.shape), g_ln[0], g_ln[1], grad_w_qkv, gb_qkv.reshape(heads, qkv_width), grad_w_o, gb_o, g_ln[2], g_ln[3], grad_w_in, gb_in, grad_w_out, gb_out)

    return jax.shard_map(layer_block, mesh=mesh,
                         in_specs=(act_spec, vec_spec, vec_spec, mat_spec, head_spec, mat_spec, vec_spec, vec_spec, vec_spec, mat_spec, vec_spec, mat_spec, vec_spec, act_spec),
                         out_specs=(act_spec, act_spec, gvec_spec, gvec_spec, gmat_spec, ghead_spec, gmat_spec, gvec_spec, gvec_spec, gvec_spec, gmat_spec, gvec_spec, gmat_spec, gvec_spec),
                         check_vma=False)
```

time: 1750 us -> 1000 us (0.57); the launches traced: 1750 us -> 982 us
  waiting for transfers between devices: 1130 us -> 373 us
  matrix products: 343 us -> 165 us
  local copies, waits for them, and re-layouts: 47.4 us -> 116 us
  Pallas kernels: 0 us -> 67.9 us
  starting transfers between devices: 1.8 us -> 65.8 us
  other arithmetic: 128 us -> 77.8 us
    reduce_scatter x8 -> x4, waiting for transfers between devices: 737 us -> 0.08 us  [scatter_rows(): return lax.psum_scatter(part, 'row', scatter_dimension=0, tiled=True)]
    all_gather x8 -> x4, waiting for transfers between devices: 386 us -> 6.7 us  [gather_rows(): return lax.all_gather(w_blk, 'row', axis=0, tiled=True)]
    ppermute x0 -> x41, waiting for transfers between devices: none -> 364 us  [the longest x5 106 us: ring_gather(): from_low = lax.ppermute(blk, 'col', up)]
    dot_general x40 -> x18, matrix products: 343 us -> 165 us  [the longest x10 60.6 us: dot_tl(): lax.dot_general(lhs, rhs, (((0,), (0,)), ((), ())), preferred_element_typ...]
    pallas_call x0 -> x2, Pallas kernels: none -> 67.9 us  [the longest x1 42 us: attention_bwd(): pl.pallas_call(functools.partial(attn_bwd_kernel, head_dim ** (-0.5), min...]
    ppermute x0 -> x41, starting transfers between devices: none -> 65.3 us  [the longest x5 11.6 us: ring_gather(): from_high = lax.ppermute(blk, 'col', down)]
    mul x4 -> x0, other arithmetic: 50.7 us -> none  [attend_one(): scores * head_dim ** (-0.5)]
    dynamic_update_slice x0 -> x30, local copies, waits for them, and re-layouts: none -> 36.5 us  [the longest x23 33.1 us: place(): return lax.dynamic_update_slice(whole, part, tuple(offs))]
  transfers between devices with their start and end apart: 16 -> 49, of which waited for: 12 -> 22; matrix products, arithmetic and copies ran while one was open for 25% -> 29% of each run, Pallas kernels for 0% -> 7%
where the time goes in v1:
time: 1000 us; the launch traced here: 982 us
  waiting for transfers between devices  373 us (37%)
  matrix products  165 us (16%)
  local copies, waits for them, and re-layouts  116 us (12%)
  blocking collectives  101 us (10%)
  other arithmetic  77.8 us (8%)
  Pallas kernels  67.9 us (7%)
  starting transfers between devices  65.8 us (7%)
  between operations  15.7 us (2%)
    ppermute x5, waiting for transfers between devices, ring_gather(): from_low = lax.ppermute(blk, 'col', up)  106 us
    ppermute x3, waiting for transfers between devices, ring_scatter(): lax.ppermute(jnp.concatenate([low[:half], low[half:] + from_high], axis=0...  91.3 us
    dot_general x10, matrix products, dot_tl(): lax.dot_general(lhs, rhs, (((0,), (0,)), ((), ())), preferred_element_typ...  60.6 us
    dot_general x5, matrix products, dot(): return jnp.dot(lhs, rhs, preferred_element_type=F32)  59.3 us
    psum x1, blocking collectives, layer_block(): lax.psum(jnp.stack([ln1_gscale, ln1_gshift, ln2_gscale, ln2_gshift]), ('c...  45.9 us
    dot_general x3, matrix products, dot_tr(): lax.dot_general(lhs, rhs, (((1,), (1,)), ((), ())), preferred_element_typ...  44.7 us
    psum x1, blocking collectives, layer_block(): lax.psum(jnp.concatenate([tok_sum(grad_pre), tok_sum(g_loc), tok_sum(own_...  43 us
    pallas_call x1, Pallas kernels, attention_bwd(): pl.pallas_call(functools.partial(attn_bwd_kernel, head_dim ** (-0.5), min...  42 us
  transfers between devices with their start and end apart: 49, of which 22 were waited for; matrix products, arithmetic and copies ran while one was open for 29% of the time, Pallas kernels for 7%

profile of v1, /device:TPU:96, one launch (start us, length us, event | category | flops | bytes accessed | tf_op | source)
XLA Modules:
  0.0 981.9 jit_solution(3227817701144960173)
XLA Ops:
  11.5 34.4 %collective-permute-done = bf16[2048,384]{1,0:T(8,128)(2,1)S(1)} collective-permute-done((bf16[2048,384]{1,0:T(8,128)(2,1)}, bf16[2048,384]{1,0:T(8,128)(2,1)S(1)}, u32[]{:S(2)}, u32[]{:S(2)}) %collective-permute-start) | collective-permute-done | bytes 1572896 | tf_op jit(solution)/shard_map/ppermute | solution.py:191
  58.3 8.5 collective-permute-done.2
  73.2 11.9 %all_gather.15 = f32[1536,5]{0,1:T(8,128)S(1)} all-gather(f32[384,5]{0,1:T(8,128)S(1)} %stack.50), channel_id=1, replica_groups=mesh['dp'=1,'col'=4,'row'=8] {'col'}, dimensions={0}, use_global_device_ids=true | all-gather | bytes 38400 | tf_op jit(solution)/shard_map/all_gather | solution.py:261
  85.7 6.7 all-gather.7.cloned.1.call-done
  111.6 32.8 %collective-permute-done.7 = bf16[1536,384]{1,0:T(8,128)(2,1)S(1)} collective-permute-done((bf16[1536,384]{1,0:T(8,128)(2,1)}, bf16[1536,384]{1,0:T(8,128)(2,1)S(1)}, u32[]{:S(2)}, u32[]{:S(2)}) %collective-permute-start.7) | collective-permute-done | bytes 1179680 | tf_op jit(solution)/shard_map/ppermute | solution.py:191
  156.9 13.8 %add_convert_fusion.q_ref.k_ref.v_ref = bf16[2048,1536]{1,0:T(8,128)(2,1)} fusion(bf16[1536,1536]{0,1:T(8,128)(2,1)S(1)} %bitcast.85, f32[1536]{0:T(1024)S(1)} %copy-done.36, bf16[2048,1536]{1,0:T(8,128)(2,1)} %constant_dynamic-update-slice_fusion.26, f32[1536]{0:T(1024)S(1)} %copy-done.32, f32[1536]{0:T(1024)S(1)} %get-tuple-element.86, ...), kind=kOutput, calls=%fused_computation.30 | convolution fusion | flops 9688842240 | bytes 17336320 | tf_op jit(solution)/shard_map/dot_general | solution.py:22
  170.7 25.9 %attn_fwd.1 = (bf16[2048,512]{1,0:T(8,128)(2,1)S(1)}, f32[4,1,2048]{2,1,0:T(1,128)S(1)}, f32[4,1,2048]{2,1,0:T(1,128)S(1)}) custom-call(bf16[2048,1536]{1,0:T(8,128)(2,1)} %add_convert_fusion.q_ref.k_ref.v_ref, bf16[2048,1536]{1,0:T(8,128)(2,1)} %add_convert_fusion.q_ref.k_ref.v_ref, bf16[2048,1536]{1,0:T(8,128)(2,1)} %add_convert_fusion.q_ref.k_ref.v_ref), custom_call_target="tpu_custom_call" | custom-call | flops 34359738368 | bytes 9437184 | tf_op jit(solution)/shard_map/attn_fwd/pallas_call | solution.py:111
  211.2 8.8 collective-permute-done.4
  237.7 19.7 %collective-permute-done.16 = bf16[2048,384]{1,0:T(8,128)(2,1)S(1)} collective-permute-done((bf16[2048,384]{1,0:T(8,128)(2,1)}, bf16[2048,384]{1,0:T(8,128)(2,1)S(1)}, u32[]{:S(2)}, u32[]{:S(2)}) %collective-permute-start.16) | collective-permute-done | bytes 1572896 | tf_op jit(solution)/shard_map/ppermute | solution.py:192
  261.9 9.7 collective-permute-done.11
  272.9 15.6 %collective-permute-done.17 = bf16[1024,384]{1,0:T(8,128)(2,1)S(1)} collective-permute-done((bf16[1024,384]{1,0:T(8,128)(2,1)S(1)}, bf16[1024,384]{1,0:T(8,128)(2,1)S(1)}, u32[]{:S(2)}, u32[]{:S(2)}) %collective-permute-start.17) | collective-permute-done | bytes 786464 | tf_op jit(solution)/shard_map/ppermute | solution.py:193
  288.6 16.4 %collective-permute-done.18 = bf16[1024,384]{1,0:T(8,128)(2,1)S(1)} collective-permute-done((bf16[1024,384]{1,0:T(8,128)(2,1)S(1)}, bf16[1024,384]{1,0:T(8,128)(2,1)S(1)}, u32[]{:S(2)}, u32[]{:S(2)}) %collective-permute-start.18) | collective-permute-done | bytes 786464 | tf_op jit(solution)/shard_map/ppermute | solution.py:194
  315.9 10.5 %collective-permute-done.14 = bf16[256,1536]{1,0:T(8,128)(2,1)S(1)} collective-permute-done((bf16[256,1536]{1,0:T(8,128)(2,1)S(1)}, bf16[256,1536]{1,0:T(8,128)(2,1)S(1)}, u32[]{:S(2)}, u32[]{:S(2)}) %collective-permute-start.14) | collective-permute-done | bytes 786464 | tf_op jit(solution)/shard_map/ppermute | solution.py:194
  332.1 18.6 %multiply_convert_fusion = (bf16[2048,1536]{1,0:T(8,128)(2,1)S(1)}, f32[2048,1536]{1,0:T(8,128)}) fusion(f32[1536]{0:T(1024)S(1)} %copy-done.49, bf16[1536,1536]{1,0:T(8,128)(2,1)} %all-gather.11.cloned.1.call-done, bf16[2048,1536]{1,0:T(8,128)(2,1)} %constant_dynamic-update-slice_fusion.9, f32[1536]{0:T(1024)S(1)} %copy-done.34, ...), kind=kOutput, calls=%fused_computation.29 | convolution fusion | flops 9714008064 | bytes 29919232 | tf_op jit(solution)/shard_map/dot_general | solution.py:22
  368.9 22.8 %fusion.76 = (f32[1536]{0:T(1024)}, bf16[2048,1536]{1,0:T(8,128)(2,1)}) fusion(f32[2048,1536]{1,0:T(8,128)} %get-tuple-element.131, f32[1536]{0:T(1024)S(1)} %copy-done.49, bf16[2048,1536]{1,0:T(8,128)(2,1)S(1)} %bitcast.71, bf16[1536,1536]{1,0:T(8,128)(2,1)} %bitcast.83), kind=kOutput, calls=%fused_computation.196 | convolution fusion | flops 9739171840 | bytes 29896704 | tf_op jit(solution)/shard_map/dot_general | solution.py:26
  391.7 13.4 %fusion.46 = f32[2048,1536]{1,0:T(8,128)S(1)} fusion(bf16[1536,1536]{1,0:T(8,128)(2,1)} %all-gather.11.cloned.1.call-done, bf16[2048,1536]{1,0:T(8,128)(2,1)} %get-tuple-element.133), kind=kOutput, calls=%fused_computation.86 | convolution fusion | flops 9663676416 | bytes 23592960 | tf_op jit(solution)/shard_map/dot_general | solution.py:26
  409.8 9.3 fusion.52
  429.0 13.8 %collective-permute-done.20 = f32[256,1536]{1,0:T(8,128)S(1)} collective-permute-done((f32[256,1536]{1,0:T(8,128)S(1)}, f32[256,1536]{1,0:T(8,128)S(1)}, u32[]{:S(2)}, u32[]{:S(2)}) %collective-permute-start.20) | collective-permute-done | bytes 1572896 | tf_op jit(solution)/shard_map/ppermute | solution.py:216
  455.4 16.0 %fusion.77 = f32[2048,1536]{1,0:T(8,128)} fusion(bf16[2048,1536]{1,0:T(8,128)(2,1)} %copy-done.50, bf16[1536,1536]{1,0:T(8,128)(2,1)} %bitcast.84), kind=kOutput, calls=%fused_computation.197 | convolution fusion | flops 9663676416 | bytes 23592960 | tf_op jit(solution)/shard_map/dot_general | solution.py:22
  471.4 42.0 %collective-permute-done.23 = f32[512,1536]{1,0:T(8,128)} collective-permute-done((f32[512,1536]{1,0:T(8,128)S(1)}, f32[512,1536]{1,0:T(8,128)}, u32[]{:S(2)}, u32[]{:S(2)}) %collective-permute-start.23) | collective-permute-done | bytes 3145760 | tf_op jit(solution)/shard_map/ppermute | solution.py:221
  539.8 28.8 %collective-permute-done.24 = bf16[512,1536]{1,0:T(8,128)(2,1)S(1)} collective-permute-done((bf16[512,1536]{1,0:T(8,128)(2,1)}, bf16[512,1536]{1,0:T(8,128)(2,1)S(1)}, u32[]{:S(2)}, u32[]{:S(2)}) %collective-permute-start.24) | collective-permute-done | bytes 1572896 | tf_op jit(solution)/shard_map/ppermute | solution.py:191
  569.5 16.0 %fusion.44 = f32[1536,1536]{1,0:T(8,128)} fusion(bf16[2048,1536]{1,0:T(8,128)(2,1)} %get-tuple-element.133, bf16[2048,1536]{1,0:T(8,128)(2,1)} %constant_dynamic-update-slice_fusion.9, f32[1536]{0:T(1024)S(1)} %copy-done.34, f32[1536]{0:T(1024)S(1)} %get-tuple-element.82, f32[2048]{0:T(1024)S(1)} %get-tuple-element.121, f32[2048]{0:T(1024)S(1)} %get-tuple-element.120), kind=kOutput, calls=%fused_computation.84 | convolution fusion | flops 9682550784 | bytes 22048768 | tf_op jit(solution)/shard_map/dot_general | solution.py:30
  593.5 8.5 collective-permute-done.27
  615.8 42.0 %attn_bwd.1 = (bf16[2048,512]{1,0:T(8,128)(2,1)S(1)}, bf16[2048,512]{1,0:T(8,128)(2,1)S(1)}, bf16[2048,512]{1,0:T(8,128)(2,1)}) custom-call(bf16[2048,1536]{1,0:T(8,128)(2,1)} %add_convert_fusion.q_ref.k_ref.v_ref, bf16[2048,1536]{1,0:T(8,128)(2,1)} %add_convert_fusion.q_ref.k_ref.v_ref, bf16[2048,1536]{1,0:T(8,128)(2,1)} %add_convert_fusion.q_ref.k_ref.v_ref, ...), custom_call_target="tpu_custom_call" | custom-call | flops 85899345920 | bytes 12582912 | tf_op jit(solution)/shard_map/attn_bwd/pallas_call | solution.py:129
  677.5 8.5 fusion.78
  691.5 27.3 %collective-permute-done.32 = f32[256,1536]{1,0:T(8,128)S(1)} collective-permute-done((f32[256,1536]{1,0:T(8,128)S(1)}, f32[256,1536]{1,0:T(8,128)S(1)}, u32[]{:S(2)}, u32[]{:S(2)}) %collective-permute-start.32) | collective-permute-done | bytes 1572896 | tf_op jit(solution)/shard_map/ppermute | solution.py:216
  736.0 15.2 %fusion.70 = f32[1536,1152]{1,0:T(8,128)} fusion(bf16[2048,1152]{0,1:T(8,128)(2,1)} %bitcast.64, bf16[2048,1536]{1,0:T(8,128)(2,1)} %constant_dynamic-update-slice_fusion.26, f32[1536]{0:T(1024)S(1)} %copy-done.33, f32[1536]{0:T(1024)S(1)} %copy-done.29, f32[2048]{0:T(1024)S(1)} %copy-done.40, f32[2048]{0:T(1024)S(1)} %copy-done.38), kind=kOutput, calls=%fused_computation.193 | convolution fusion | flops 7266631680 | bytes 18116608 | tf_op jit(solution)/shard_map/dot_general | solution.py:30
  751.2 41.3 %collective-permute-done.35 = f32[512,1536]{1,0:T(8,128)} collective-permute-done((f32[512,1536]{1,0:T(8,128)}, f32[512,1536]{1,0:T(8,128)}, u32[]{:S(2)}, u32[]{:S(2)}) %collective-permute-start.35) | collective-permute-done | bytes 3145760 | tf_op jit(solution)/shard_map/ppermute | solution.py:221
  821.7 43.0 %psum.15 = f32[3456]{0:T(1024)S(1)} all-reduce(f32[3456]{0:T(1024)S(1)} %pad_maximum_fusion.10), channel_id=1, replica_groups=mesh['dp'=1,'col'=4,'row'=8] {'row'}, use_global_device_ids=true, to_apply=%region_24.25 | all-reduce | flops 3456 | bytes 27648 | tf_op jit(solution)/shard_map/psum | solution.py:359
  873.9 8.1 collective-permute-done.31
  882.0 23.7 %collective-permute-done.30 = f32[2048,384]{1,0:T(8,128)} collective-permute-done((f32[2048,384]{1,0:T(8,128)}, f32[2048,384]{1,0:T(8,128)}, u32[]{:S(2)}, u32[]{:S(2)}) %collective-permute-start.30) | collective-permute-done | bytes 3145760 | tf_op jit(solution)/shard_map/ppermute | solution.py:220
  917.7 45.9 %psum.14 = f32[4,1536]{1,0:T(4,128)S(1)} all-reduce(f32[4,1536]{1,0:T(4,128)S(1)} %pad_maximum_fusion.9), channel_id=1, replica_groups=mesh['dp'=1,'col'=4,'row'=8] {'col','row'}, use_global_device_ids=true, to_apply=%region_18.19 | all-reduce | flops 6144 | bytes 49152 | tf_op jit(solution)/shard_map/psum | solution.py:362
  (339 shorter events, 307.4 us)
Async XLA Ops:
  7.2 85.2 %all-gather.7.cloned.1.call-start = ((), (), s32[]{:S(2)}) async-start(), calls=%async_computation.5 | async-start | bytes 1327104 | tf_op jit(solution)/shard_map/all_gather | solution.py:258
  7.3 38.6 %collective-permute-start = (bf16[2048,384]{1,0:T(8,128)(2,1)}, bf16[2048,384]{1,0:T(8,128)(2,1)S(1)}, u32[]{:S(2)}, u32[]{:S(2)}) collective-permute-start(bf16[2048,384]{1,0:T(8,128)(2,1)} %bitcast.87), channel_id=1, source_target_pairs={{0,8},{8,16},{16,24},{24,0},{1,9},{9,17},{17,25},{25,1},{2,10},{10... | collective-permute-start | bytes 4718600 | tf_op jit(solution)/shard_map/ppermute | solution.py:191
  71.2 80.6 %all-gather.5.cloned.1.call-start = ((), (), s32[]{:S(2)}) async-start(), calls=%async_computation.4 | async-start | bytes 3981312 | tf_op jit(solution)/shard_map/all_gather | solution.py:258
  72.0 260.0 %all-gather.11.cloned.1.call-start = ((), (), s32[]{:S(2)}) async-start(), calls=%async_computation.7 | async-start | bytes 5308416 | tf_op jit(solution)/shard_map/all_gather | solution.py:258
  72.8 286.8 %all-gather.9.cloned.1.call-start = ((), (), s32[]{:S(2)}) async-start(), calls=%async_computation.6 | async-start | bytes 5308416 | tf_op jit(solution)/shard_map/all_gather | solution.py:258
  92.4 52.1 %collective-permute-start.7 = (bf16[1536,384]{1,0:T(8,128)(2,1)}, bf16[1536,384]{1,0:T(8,128)(2,1)S(1)}, u32[]{:S(2)}, u32[]{:S(2)}) collective-permute-start(bf16[1536,384]{1,0:T(8,128)(2,1)} %all-gather.7.cloned.1.call-done), channel_id=1, source_target_pairs={{0,8},{8,16},{16,24},{24,0},{1,9},{9,17},{17,25},{25,1},{2,10},{10... | collective-permute-start | bytes 3538952 | tf_op jit(solution)/shard_map/ppermute | solution.py:191
  93.9 54.0 %collective-permute-start.8 = (bf16[1536,384]{1,0:T(8,128)(2,1)}, bf16[1536,384]{1,0:T(8,128)(2,1)S(1)}, u32[]{:S(2)}, u32[]{:S(2)}) collective-permute-start(bf16[1536,384]{1,0:T(8,128)(2,1)} %all-gather.7.cloned.1.call-done), channel_id=1, source_target_pairs={{0,24},{8,0},{16,8},{24,16},{1,25},{9,1},{17,9},{25,17},{2,26},{10... | collective-permute-start | bytes 3538952 | tf_op jit(solution)/shard_map/ppermute | solution.py:192
  96.3 140.1 %collective-permute-start.15 = (bf16[2048,384]{1,0:T(8,128)(2,1)}, bf16[2048,384]{1,0:T(8,128)(2,1)}, u32[]{:S(2)}, u32[]{:S(2)}) collective-permute-start(bf16[2048,384]{1,0:T(8,128)(2,1)} %bitcast), channel_id=1, source_target_pairs={{0,8},{8,16},{16,24},{24,0},{1,9},{9,17},{17,25},{25,1},{2,10},{10... | collective-permute-start | bytes 4718600 | tf_op jit(solution)/shard_map/ppermute | solution.py:191
  107.8 507.9 %reduce-scatter.5.cloned.1.call-start = ((), (), s32[]{:S(2)}) async-start(), calls=%async_computation.8 | async-start | bytes 10616832 | tf_op jit(solution)/shard_map/reduce_scatter | solution.py:264
  145.3 60.4 %collective-permute-start.9 = (bf16[768,384]{1,0:T(8,128)(2,1)}, bf16[768,384]{1,0:T(8,128)(2,1)}, u32[]{:S(2)}, u32[]{:S(2)}) collective-permute-start(bf16[768,384]{1,0:T(8,128)(2,1)} %slice.209), channel_id=1, source_target_pairs={{0,8},{8,16},{16,24},{24,0},{1,9},{9,17},{17,25},{25,1},{2,10},{10... | collective-permute-start | bytes 1769480 | tf_op jit(solution)/shard_map/ppermute | solution.py:193
  148.8 59.6 %collective-permute-start.10 = (bf16[768,384]{1,0:T(8,128)(2,1)}, bf16[768,384]{1,0:T(8,128)(2,1)}, u32[]{:S(2)}, u32[]{:S(2)}) collective-permute-start(bf16[768,384]{1,0:T(8,128)(2,1)} %slice.210), channel_id=1, source_target_pairs={{0,24},{8,0},{16,8},{24,16},{1,25},{9,1},{17,9},{25,17},{2,26},{10... | collective-permute-start | bytes 1769480 | tf_op jit(solution)/shard_map/ppermute | solution.py:194
  208.4 49.0 %collective-permute-start.16 = (bf16[2048,384]{1,0:T(8,128)(2,1)}, bf16[2048,384]{1,0:T(8,128)(2,1)S(1)}, u32[]{:S(2)}, u32[]{:S(2)}) collective-permute-start(bf16[2048,384]{1,0:T(8,128)(2,1)} %bitcast), channel_id=1, source_target_pairs={{0,24},{8,0},{16,8},{24,16},{1,25},{9,1},{17,9},{25,17},{2,26},{10... | collective-permute-start | bytes 4718600 | tf_op jit(solution)/shard_map/ppermute | solution.py:192
  233.1 72.1 %collective-permute-start.12 = (bf16[512,1536]{1,0:T(8,128)(2,1)S(1)}, bf16[512,1536]{1,0:T(8,128)(2,1)}, u32[]{:S(2)}, u32[]{:S(2)}) collective-permute-start(bf16[512,1536]{1,0:T(8,128)(2,1)S(1)} %get-tuple-element.129), channel_id=1, source_target_pairs={{0,24},{8,0},{16,8},{24,16},{1,25},{9,1},{17,9},{25,17},{2,26},{10... | collective-permute-start | bytes 4718600 | tf_op jit(solution)/shard_map/ppermute | solution.py:192
  237.6 50.9 %collective-permute-start.17 = (bf16[1024,384]{1,0:T(8,128)(2,1)S(1)}, bf16[1024,384]{1,0:T(8,128)(2,1)S(1)}, u32[]{:S(2)}, u32[]{:S(2)}) collective-permute-start(bf16[1024,384]{1,0:T(8,128)(2,1)S(1)} %slice.214), channel_id=1, source_target_pairs={{0,8},{8,16},{16,24},{24,0},{1,9},{9,17},{17,25},{25,1},{2,10},{10... | collective-permute-start | bytes 2359304 | tf_op jit(solution)/shard_map/ppermute | solution.py:193
  257.5 47.5 %collective-permute-start.18 = (bf16[1024,384]{1,0:T(8,128)(2,1)S(1)}, bf16[1024,384]{1,0:T(8,128)(2,1)S(1)}, u32[]{:S(2)}, u32[]{:S(2)}) collective-permute-start(bf16[1024,384]{1,0:T(8,128)(2,1)S(1)} %slice.215), channel_id=1, source_target_pairs={{0,24},{8,0},{16,8},{24,16},{1,25},{9,1},{17,9},{25,17},{2,26},{10... | collective-permute-start | bytes 2359304 | tf_op jit(solution)/shard_map/ppermute | solution.py:194
  272.8 42.2 %collective-permute-start.13 = (bf16[256,1536]{1,0:T(8,128)(2,1)S(1)}, bf16[256,1536]{1,0:T(8,128)(2,1)S(1)}, u32[]{:S(2)}, u32[]{:S(2)}) collective-permute-start(bf16[256,1536]{1,0:T(8,128)(2,1)S(1)} %slice.212), channel_id=1, source_target_pairs={{0,8},{8,16},{16,24},{24,0},{1,9},{9,17},{17,25},{25,1},{2,10},{10... | collective-permute-start | bytes 2359304 | tf_op jit(solution)/shard_map/ppermute | solution.py:193
  444.1 69.3 %collective-permute-start.23 = (f32[512,1536]{1,0:T(8,128)S(1)}, f32[512,1536]{1,0:T(8,128)}, u32[]{:S(2)}, u32[]{:S(2)}) collective-permute-start(f32[512,1536]{1,0:T(8,128)S(1)} %pad_maximum_fusion.3), channel_id=1, source_target_pairs={{0,24},{8,0},{16,8},{24,16},{1,25},{9,1},{17,9},{25,17},{2,26},{10... | collective-permute-start | bytes 9437192 | tf_op jit(solution)/shard_map/ppermute | solution.py:221
  449.5 69.3 %collective-permute-start.21 = (f32[512,1536]{1,0:T(8,128)}, f32[512,1536]{1,0:T(8,128)}, u32[]{:S(2)}, u32[]{:S(2)}) collective-permute-start(f32[512,1536]{1,0:T(8,128)} %pad_maximum_fusion.2), channel_id=1, source_target_pairs={{0,8},{8,16},{16,24},{24,0},{1,9},{9,17},{17,25},{25,1},{2,10},{10... | collective-permute-start | bytes 9437192 | tf_op jit(solution)/shard_map/ppermute | solution.py:220
  523.5 278.1 %reduce-scatter.7.cloned.1.call-start = ((), (), s32[]{:S(2)}) async-start(), calls=%async_computation.9 | async-start | bytes 10616832 | tf_op jit(solution)/shard_map/reduce_scatter | solution.py:264
  536.6 48.9 %collective-permute-start.25 = (bf16[512,1536]{1,0:T(8,128)(2,1)}, bf16[512,1536]{1,0:T(8,128)(2,1)S(1)}, u32[]{:S(2)}, u32[]{:S(2)}) collective-permute-start(bf16[512,1536]{1,0:T(8,128)(2,1)} %get-tuple-element.92), channel_id=1, source_target_pairs={{0,24},{8,0},{16,8},{24,16},{1,25},{9,1},{17,9},{25,17},{2,26},{10... | collective-permute-start | bytes 4718600 | tf_op jit(solution)/shard_map/ppermute | solution.py:192
  606.8 68.6 %collective-permute-start.28 = (f32[1024,384]{1,0:T(8,128)}, f32[1024,384]{1,0:T(8,128)}, u32[]{:S(2)}, u32[]{:S(2)}) collective-permute-start(f32[1024,384]{1,0:T(8,128)} %get-tuple-element.104), channel_id=1, source_target_pairs={{0,8},{8,16},{16,24},{24,0},{1,9},{9,17},{17,25},{25,1},{2,10},{10... | collective-permute-start | bytes 4718600 | tf_op jit(solution)/shard_map/ppermute | solution.py:216
  606.8 68.6 %collective-permute-start.29 = (f32[1024,384]{1,0:T(8,128)}, f32[1024,384]{1,0:T(8,128)}, u32[]{:S(2)}, u32[]{:S(2)}) collective-permute-start(f32[1024,384]{1,0:T(8,128)} %get-tuple-element.103), channel_id=1, source_target_pairs={{0,24},{8,0},{16,8},{24,16},{1,25},{9,1},{17,9},{25,17},{2,26},{10... | collective-permute-start | bytes 4718600 | tf_op jit(solution)/shard_map/ppermute | solution.py:217
  615.7 351.0 %reduce-scatter.11.cloned.1.call-start = ((), (), s32[]{:S(2)}) async-start(), calls=%async_computation.11 | async-start | bytes 2654208 | tf_op jit(solution)/shard_map/reduce_scatter | solution.py:264
  728.3 64.2 %collective-permute-start.35 = (f32[512,1536]{1,0:T(8,128)}, f32[512,1536]{1,0:T(8,128)}, u32[]{:S(2)}, u32[]{:S(2)}) collective-permute-start(f32[512,1536]{1,0:T(8,128)} %pad_maximum_fusion.7), channel_id=1, source_target_pairs={{0,24},{8,0},{16,8},{24,16},{1,25},{9,1},{17,9},{25,17},{2,26},{10... | collective-permute-start | bytes 9437192 | tf_op jit(solution)/shard_map/ppermute | solution.py:221
  731.9 65.1 %collective-permute-start.33 = (f32[512,1536]{1,0:T(8,128)}, f32[512,1536]{1,0:T(8,128)}, u32[]{:S(2)}, u32[]{:S(2)}) collective-permute-start(f32[512,1536]{1,0:T(8,128)} %pad_maximum_fusion.6), channel_id=1, source_target_pairs={{0,8},{8,16},{16,24},{24,0},{1,9},{9,17},{17,25},{25,1},{2,10},{10... | collective-permute-start | bytes 9437192 | tf_op jit(solution)/shard_map/ppermute | solution.py:220
  801.7 167.8 %reduce-scatter.9.cloned.1.call-start = ((), (), s32[]{:S(2)}) async-start(), calls=%async_computation.10 | async-start | bytes 7962624 | tf_op jit(solution)/shard_map/reduce_scatter | solution.py:264
  808.6 73.4 %collective-permute-start.31 = (f32[2048,384]{1,0:T(8,128)}, f32[2048,384]{1,0:T(8,128)}, u32[]{:S(2)}, u32[]{:S(2)}) collective-permute-start(f32[2048,384]{1,0:T(8,128)} %pad_maximum_fusion.5), channel_id=1, source_target_pairs={{0,24},{8,0},{16,8},{24,16},{1,25},{9,1},{17,9},{25,17},{2,26},{10... | collective-permute-start | bytes 9437192 | tf_op jit(solution)/shard_map/ppermute | solution.py:221
  810.5 95.3 %collective-permute-start.30 = (f32[2048,384]{1,0:T(8,128)}, f32[2048,384]{1,0:T(8,128)}, u32[]{:S(2)}, u32[]{:S(2)}) collective-permute-start(f32[2048,384]{1,0:T(8,128)} %pad_maximum_fusion.4), channel_id=1, source_target_pairs={{0,8},{8,16},{16,24},{24,0},{1,9},{9,17},{17,25},{25,1},{2,10},{10... | collective-permute-start | bytes 9437192 | tf_op jit(solution)/shard_map/ppermute | solution.py:220
  818.0 48.6 %collective-permute-start.40 = (bf16[768,384]{1,0:T(8,128)(2,1)S(1)}, bf16[768,384]{1,0:T(8,128)(2,1)S(1)}, u32[]{:S(2)}, u32[]{:S(2)}) collective-permute-start(bf16[768,384]{1,0:T(8,128)(2,1)S(1)} %convert_element_type.126), channel_id=1, source_target_pairs={{0,0},{8,2},{16,4},{24,6},{1,1},{9,3},{17,5},{25,7},{2,8},{10,10},... | collective-permute-start | bytes 1769480 | tf_op jit(solution)/shard_map/ppermute | solution.py:279
  873.9 90.7 %collective-permute-start.36 = (bf16[512,384]{1,0:T(8,128)(2,1)}, bf16[512,384]{1,0:T(8,128)(2,1)}, u32[]{:S(2)}, u32[]{:S(2)}) collective-permute-start(bf16[512,384]{1,0:T(8,128)(2,1)} %get-tuple-element.113), channel_id=1, source_target_pairs={{0,8},{8,16},{16,24},{24,0},{1,9},{9,17},{17,25},{25,1},{2,10},{10... | collective-permute-start | bytes 1179656 | tf_op jit(solution)/shard_map/ppermute | solution.py:237
  911.6 54.0 %collective-permute-start.37 = (bf16[512,384]{1,0:T(8,128)(2,1)}, bf16[512,384]{1,0:T(8,128)(2,1)}, u32[]{:S(2)}, u32[]{:S(2)}) collective-permute-start(bf16[512,384]{1,0:T(8,128)(2,1)} %get-tuple-element.112), channel_id=1, source_target_pairs={{0,16},{8,24},{16,0},{24,8},{1,17},{9,25},{17,1},{25,9},{2,18},{10... | collective-permute-start | bytes 1179656 | tf_op jit(solution)/shard_map/ppermute | solution.py:237
  911.6 56.8 %collective-permute-start.38 = (bf16[512,384]{1,0:T(8,128)(2,1)S(1)}, bf16[512,384]{1,0:T(8,128)(2,1)}, u32[]{:S(2)}, u32[]{:S(2)}) collective-permute-start(bf16[512,384]{1,0:T(8,128)(2,1)S(1)} %get-tuple-element.111), channel_id=1, source_target_pairs={{0,24},{8,0},{16,8},{24,16},{1,25},{9,1},{17,9},{25,17},{2,26},{10... | collective-permute-start | bytes 1179656 | tf_op jit(solution)/shard_map/ppermute | solution.py:237
  (74 other events, 968.8 us)
Sparse Core Ops, SparseCore 0:
  71.3 20.9 all-gather.6
  93.9 50.7 all-gather.4
  146.3 27.7 all-gather.10
  175.6 31.4 all-gather.8
  523.6 51.8 reduce-scatter.4
  615.8 53.1 reduce-scatter.6
  801.8 44.4 reduce-scatter.10
  848.6 43.8 reduce-scatter.8

commit v2 on v1

--- a/solution.py
+++ b/solution.py
@@ -58,7 +58,8 @@
         r_ref[0, :, rows] = recip
 
 
-def attn_bwd_kernel(scale, blk, q_ref, k_ref, v_ref, do_ref, m_ref, r_ref, dq_ref, dk_ref, dv_ref, dk_acc, dv_acc):
+def attn_bwd_kernel(scale, blk, q_ref, k_ref, v_ref, do_ref, m_ref, r_ref, *rest):
+    grad_ref, dk_acc, dv_acc = rest[-3:]
     seq_len = q_ref.shape[0]
     keys_t = k_ref[...].astype(F32).T.astype(BF16)
     key_pos = lax.broadcasted_iota(jnp.int32, (blk, blk), 0)
@@ -93,9 +94,9 @@
             dk_acc[span, :] += dot(gscores, query)
             term = dot(keys_t[:, lo:hi], gscores)
             dq_t = term if dq_t is None else dq_t + term
-        dq_ref[rows, :] = dq_t.T.astype(BF16)
-    dk_ref[...] = dk_acc[...].astype(BF16)
-    dv_ref[...] = dv_acc[...].astype(BF16)
+        grad_ref[rows, 0:LANES] = dq_t.T.astype(BF16)
+    grad_ref[:, LANES:2 * LANES] = dk_acc[...].astype(BF16)
+    grad_ref[:, 2 * LANES:] = dv_acc[...].astype(BF16)
 
 
 def attn_specs(seq_len, part):
@@ -120,23 +121,30 @@
     )(qkv_pad, qkv_pad, qkv_pad)
 
 
-def attention_bwd(qkv_pad, grad_pad, tops, recips, seq_count, heads, head_dim):
+def attention_bwd(qkv_pad, grad_pad, tops, recips, seq_count, heads, head_dim, first, count, partial=None):
     seq_len = qkv_pad.shape[0] // seq_count
-    items = seq_count * heads
-    head_spec = pl.BlockSpec((seq_len, LANES), lambda i, h: (i, h))
-    stat_spec = pl.BlockSpec((1, 1, seq_len), lambda i, h: (i * heads + h, 0, 0))
-    flops = items * 10 * seq_len * seq_len * LANES // 2
+    stat_spec = pl.BlockSpec((1, 1, seq_len), lambda i, h: (i * heads + first + h, 0, 0))
+    in_specs = [pl.BlockSpec((seq_len, LANES), lambda i, h, part=part: (i, 3 * (first + h) + part)) for part in range(3)]
+    in_specs += [pl.BlockSpec((seq_len, LANES), lambda i, h: (i, first + h)), stat_spec, stat_spec]
+    operands = [qkv_pad, qkv_pad, qkv_pad, grad_pad, tops, recips]
+    aliases = {}
+    if partial is not None:
+        aliases = {len(operands): 0}
+        in_specs.append(pl.BlockSpec(memory_space=pl.ANY))
+        operands.append(partial)
+    flops = seq_count * count * 10 * seq_len * seq_len * LANES // 2
     return pl.pallas_call(
         functools.partial(attn_bwd_kernel, head_dim ** -0.5, min(Q_BLOCK, seq_len)),
-        grid=(seq_count, heads),
-        in_specs=[attn_specs(seq_len, part) for part in range(3)] + [head_spec, stat_spec, stat_spec],
-        out_specs=[head_spec] * 3,
-        out_shape=[jax.ShapeDtypeStruct((qkv_pad.shape[0], heads * LANES), BF16)] * 3,
+        grid=(seq_count, count),
+        in_specs=in_specs,
+        out_specs=pl.BlockSpec((seq_len, 3 * LANES), lambda i, h: (i, first + h)),
+        out_shape=jax.ShapeDtypeStruct(qkv_pad.shape, BF16),
         scratch_shapes=[pltpu.VMEM((seq_len, LANES), F32)] * 2,
-        cost_estimate=pl.CostEstimate(flops=8 * flops, bytes_accessed=qkv_pad.size * 4, transcendentals=0),
+        input_output_aliases=aliases,
+        cost_estimate=pl.CostEstimate(flops=8 * flops, bytes_accessed=qkv_pad.size * 2, transcendentals=0),
         compiler_params=pltpu.CompilerParams(vmem_limit_bytes=48 << 20),
         name="attn_bwd",
-    )(qkv_pad, qkv_pad, qkv_pad, grad_pad, tops, recips)
+    )(*operands)
 
 
 def pad_heads(arr, heads, head_dim):
@@ -172,7 +180,7 @@
     return grad_in, jnp.sum(grad_f32 * normed, axis=0), jnp.sum(grad_f32, axis=0)
 
 
-def ring_gather(blk, size, axis):
+def ring_gather(blk, size, axis, between=None, after=None):
     me = lax.axis_index('col')
     width = blk.shape[axis]
     up = [(i, (i + 1) % size) for i in range(size)]
@@ -190,8 +198,12 @@
     whole = place(jnp.zeros(tuple(whole_shape), blk.dtype), blk, me, 0)
     from_low = lax.ppermute(blk, 'col', up)
     from_high = lax.ppermute(blk, 'col', down)
+    if between is not None:
+        from_low, from_high = between(from_low, from_high)
     far_a = lax.ppermute(from_low[:half], 'col', up)
     far_b = lax.ppermute(from_high[half:], 'col', down)
+    if after is not None:
+        far_a, far_b = after(far_a, far_b)
     whole = place(whole, from_low, me - 1, 0)
     whole = place(whole, from_high, me + 1, 0)
     whole = place(whole, far_a, me + 2, 0)
@@ -257,16 +269,12 @@
     def gather_rows(w_blk):
         return lax.all_gather(w_blk, 'row', axis=0, tiled=True)
 
-    def gather_vec(vec):
-        return lax.all_gather(vec, 'col', axis=0, tiled=True)
-
     def scatter_rows(part):
         return lax.psum_scatter(part, 'row', scatter_dimension=0, tiled=True)
 
     def row_split_weight(w_blk):
         depth, width = w_blk.shape
-        moved = lax.ppermute(w_blk, ('col', 'row'), flip)
-        stack = gather_rows(moved).reshape(cols, per, depth, width)
+        stack = gather_rows(w_blk).reshape(cols, per, depth, width)
         return stack.transpose(1, 2, 0, 3).reshape(per * depth, cols * width)
 
     def row_split_part(lhs, rhs):
@@ -294,27 +302,40 @@
         def own_feats(arr):
             return lax.dynamic_slice_in_dim(arr, me * d_local, d_local, arr.ndim - 1)
 
-        vecs = gather_vec(jnp.stack([ln1_scale, ln1_shift, ln2_scale, ln2_shift, b_o], axis=1))
-        scale1, shift1, scale2, shift2, bias_o = [vecs[:, i] for i in range(5)]
-
+        w_out_moved = lax.ppermute(w_out, ('col', 'row'), flip)
+        vecs = ring_gather(jnp.stack([ln1_scale, ln1_shift, ln2_scale, ln2_shift, b_o]), cols, 1)
+        scale1, shift1, scale2, shift2, bias_o = [vecs[i] for i in range(5)]
         x_full = ring_gather(x_loc, cols, 1)
         w_qkv_full = gather_rows(w_qkv)
-        w_out_blk, w_o_blk, w_in_blk, g_blk, x_full = lax.optimization_barrier((w_out, w_o, w_in, g_loc, x_full))
-        w_o_full = ring_gather(gather_rows(w_o_blk), cols, 1)
-        w_out_rows = row_split_weight(w_out_blk)
-        w_in_full = gather_rows(w_in_blk)
-        g_full = ring_gather(g_blk, cols, 1)
+        w_o_cols = gather_rows(w_o)
+        w_in_full = gather_rows(w_in)
+        g_blk, w_out_moved, x_full = tie(g_loc, w_out_moved, x_full)
+        w_out_rows = row_split_weight(w_out_moved)
 
         normed1 = layer_norm(x_full, scale1, shift1)
         w_qkv_pad = pad_heads(w_qkv_full, 3 * heads, head_dim)
         b_qkv_pad = pad_heads(b_qkv.reshape(heads * qkv_width), 3 * heads, head_dim)
         qkv_pad = (dot(normed1, w_qkv_pad) + b_qkv_pad).astype(BF16)
-        o_pad, tops, recips = attention_fwd(qkv_pad, seq_count, heads, head_dim)
+
+        def under_qkv(from_low, from_high):
+            nonlocal qkv_pad, w_o_cols
+            qkv_pad, w_o_cols, from_low, from_high = tie(qkv_pad, w_o_cols, from_low, from_high)
+            return from_low, from_high
+
+        def under_attention(far_a, far_b):
+            nonlocal o_pad, tops, recips, w_o_full
+            o_pad, tops, recips = attention_fwd(qkv_pad, seq_count, heads, head_dim)
+            w_o_full = ring_gather(w_o_cols, cols, 1)
+            o_pad, far_a, far_b = tie(o_pad, far_a, far_b)
+            return far_a, far_b
+
+        o_pad = tops = recips = w_o_full = None
+        g_full = ring_gather(g_blk, cols, 1, under_qkv, under_attention)
         o_loc = unpad_heads(o_pad, heads, head_dim)
         o_tok = exchange(o_loc, cols, 0, 1)
         r1_tok = (own_tokens(x_full).astype(F32) + dot(o_tok, w_o_full) + bias_o).astype(BF16)
         grad_hidden = dot_tr(g_full, w_out_rows).astype(BF16)
-        r1_full = ring_gather(r1_tok, cols, 0)
+        r1_full, grad_hidden = tie(ring_gather(r1_tok, cols, 0), grad_hidden)
         normed2 = layer_norm(r1_full, scale2, shift2)
         pre_act = dot(normed2, w_in_full) + b_in
         hidden, gelu_back = jax.vjp(gelu_tanh, pre_act)
@@ -323,45 +344,55 @@
         grad_pre_bf = grad_pre.astype(BF16)
 
         gh2 = ring_scatter(dot_tr(grad_pre_bf, w_in_full), cols, 0).astype(BF16)
-        gh2, part_w_out, out_part = tie(gh2, row_split_part(hidden, g_full), dot(hidden, w_out_rows))
+        part_w_out, out_part = row_split_part(hidden, g_full), dot(hidden, w_out_rows)
+        gh2, part_w_out, out_part = tie(gh2, part_w_out, out_part)
         ln2_grad, ln2_gscale, ln2_gshift = layer_norm_bwd(gh2, r1_tok, scale2)
         gr1_tok = (own_tokens(g_full).astype(F32) + ln2_grad).astype(BF16)
         gr1_full = ring_gather(gr1_tok, cols, 0)
-        gr1_full, part_w_in, out_part = tie(gr1_full, dot_tl(normed2, grad_pre_bf), out_part)
+        part_w_in = dot_tl(normed2, grad_pre_bf)
+        gr1_full, part_w_in, out_part = tie(gr1_full, part_w_in, out_part)
         w_o_pad = pad_heads(lax.dynamic_slice_in_dim(w_o_full, me * d_local, d_local, 0).T, heads, head_dim)
         grad_o_pad = dot(gr1_full, w_o_pad).astype(BF16)
         grad_o_pad, sum_w_out = tie(grad_o_pad, scatter_rows(part_w_out))
-        dq, dk, dv = attention_bwd(qkv_pad, grad_o_pad, tops, recips, seq_count, heads, head_dim)
-        grads = [a.reshape(tokens, heads, LANES)[..., :head_dim] for a in (dq, dk, dv)]
-        grad_qkv = jnp.stack(grads, axis=2).reshape(tokens, heads * qkv_width)
-
-        def under_attention(from_low, from_high):
-            nonlocal grad_qkv
-            grad_qkv, from_low, from_high = tie(grad_qkv, from_low, from_high)
+        part_w_o = row_split_part(tie(o_loc, grad_o_pad)[0], gr1_full)
+        grad_o_pad = tie(grad_o_pad, part_w_o)[0]
+        early_heads = max(heads // 2, 1)
+        dqkv_pad = attention_bwd(qkv_pad, grad_o_pad, tops, recips, seq_count, heads, head_dim, 0, early_heads)
+
+        def under_first_heads(from_low, from_high):
+            nonlocal dqkv_pad
+            dqkv_pad, from_low, from_high = tie(dqkv_pad, from_low, from_high)
             return from_low, from_high
 
-        out_sum = ring_scatter(out_part, cols, 1, under_attention)
+        out_sum = ring_scatter(out_part, cols, 1, under_first_heads)
+        if early_heads < heads:
+            dqkv_pad = attention_bwd(qkv_pad, grad_o_pad, tops, recips, seq_count, heads, head_dim, early_heads, heads - early_heads, dqkv_pad)
         out_rows = (own_feats(r1_full).astype(F32) + out_sum + b_out).astype(BF16)
-        gh1 = ring_scatter(dot_tr(grad_qkv, w_qkv_full), cols, 0).astype(BF16)
-        gh1, part_w_o, part_w_qkv, sum_w_in = tie(gh1, row_split_part(o_loc, gr1_full), dot_tl(normed1, grad_qkv), scatter_rows(part_w_in))
+        grad_qkv = unpad_heads(dqkv_pad, 3 * heads, head_dim)
+        gh1 = ring_scatter(dot_tr(dqkv_pad, w_qkv_pad), cols, 0).astype(BF16)
+        part_w_qkv = dot_tl(normed1, grad_qkv)
+        sum_w_in = scatter_rows(part_w_in)
+
+        def tok_sum(arr):
+            return jnp.sum(arr.astype(F32), axis=0)
+
+        ff_local = b_in.shape[0]
+        ln2_sums = ring_scatter(jnp.stack([ln2_gscale, ln2_gshift]), cols, 1)
+        early = lax.psum(jnp.concatenate([tok_sum(grad_pre), tok_sum(g_loc), tok_sum(own_feats(gr1_full)), tok_sum(grad_qkv), ln2_sums[0], ln2_sums[1]]), 'row')
+        gb_in, gb_out, gb_o, gb_qkv, g_ln2 = jnp.split(early, [ff_local, ff_local + d_local, ff_local + 2 * d_local, ff_local + 2 * d_local + heads * qkv_width])
+        g_ln2 = g_ln2.reshape(2, d_local)
+
+        gh1, part_w_qkv, _, _ = tie(gh1, part_w_qkv, sum_w_in, early)
         ln1_grad, ln1_gscale, ln1_gshift = layer_norm_bwd(gh1, own_tokens(x_full), scale1)
         gx_tok = (gr1_tok.astype(F32) + ln1_grad).astype(BF16)
         grad_x = exchange(gx_tok, cols, 1, 0)
+        g_ln1 = lax.psum(ring_scatter(jnp.stack([ln1_gscale, ln1_gshift]), cols, 1), 'row')
 
         grad_w_out = to_owner(sum_w_out)
         grad_w_in = sum_w_in.astype(BF16)
         grad_w_o = to_owner(scatter_rows(part_w_o))
         grad_w_qkv = scatter_rows(part_w_qkv).astype(BF16)
-
-        def tok_sum(arr):
-            return jnp.sum(arr.astype(F32), axis=0)
-
-        early = lax.psum(jnp.concatenate([tok_sum(grad_pre), tok_sum(g_loc), tok_sum(own_feats(gr1_full)), tok_sum(grad_qkv)]), 'row')
-        ff_local = b_in.shape[0]
-        gb_in, gb_out, gb_o, gb_qkv = jnp.split(early, [ff_local, ff_local + d_local, ff_local + 2 * d_local])
-        late = lax.psum(jnp.stack([ln1_gscale, ln1_gshift, ln2_gscale, ln2_gshift]), ('col', 'row'))
-        g_ln = own_feats(late)
-        return (out_rows.reshape(x_blk.shape), grad_x.reshape(x_blk.shape), g_ln[0], g_ln[1], grad_w_qkv, gb_qkv.reshape(heads, qkv_width), grad_w_o, gb_o, g_ln[2], g_ln[3], grad_w_in, gb_in, grad_w_out, gb_out)
+        return (out_rows.reshape(x_blk.shape), grad_x.reshape(x_blk.shape), g_ln1[0], g_ln1[1], grad_w_qkv, gb_qkv.reshape(heads, qkv_width), grad_w_o, gb_o, g_ln2[0], g_ln2[1], grad_w_in, gb_in, grad_w_out, gb_out)
 
     return jax.shard_map(layer_block, mesh=mesh,
                          in_specs=(act_spec, vec_spec, vec_spec, mat_spec, head_spec, mat_spec, vec_spec, vec_spec, vec_spec, mat_spec, vec_spec, mat_spec, vec_spec, act_spec),

time: 1000 us -> 900 us (0.900)
  blocking collectives: 101 us -> 40 us
  waiting for transfers between devices: 373 us -> 318 us
  starting transfers between devices: 65.8 us -> 93.7 us
    psum x1, blocking collectives: 45.9 us -> 13.9 us  [layer_block(): lax.psum(ring_scatter(jnp.stack([ln1_gscale, ln1_gshift]), cols, 1), 'row')]
    ppermute x3 -> x5, waiting for transfers between devices: 41.1 us -> 11.8 us  [ring_scatter(): from_low = lax.ppermute(far[:half], 'col', up)]
    ppermute x5 -> x6, waiting for transfers between devices: 35.4 us -> 11.5 us  [ring_gather(): far_b = lax.ppermute(from_high[half:], 'col', down)]
    ppermute x5 -> x6, waiting for transfers between devices: 19.8 us -> 0.05 us  [ring_gather(): from_high = lax.ppermute(blk, 'col', down)]
    psum x1, blocking collectives: 43 us -> 26 us  [layer_block(): lax.psum(jnp.concatenate([tok_sum(grad_pre), tok_sum(g_loc), tok_sum(own_...]
    ppermute x3 -> x5, waiting for transfers between devices: 0.01 us -> 16.6 us  [ring_scatter(): from_high = lax.ppermute(far[half:], 'col', down)]
    ppermute x3 -> x5, waiting for transfers between devices: 91.3 us -> 105 us  [ring_scatter(): lax.ppermute(jnp.concatenate([low[:half], low[half:] + from_high], axis=0...]
    all_gather x1 -> x0, blocking collectives: 11.9 us -> none  [gather_vec(): return lax.all_gather(vec, 'col', axis=0, tiled=True)]
  transfers between devices with their start and end apart: 49 -> 61, of which waited for: 22 -> 27; matrix products, arithmetic and copies ran while one was open for 29% -> 32% of each run, Pallas kernels for 7% -> 8%
where the time goes in v2:
time: 900 us; the launch traced here: 889 us
  waiting for transfers between devices  318 us (35%)
  matrix products  166 us (18%)
  local copies, waits for them, and re-layouts  111 us (12%)
  starting transfers between devices  93.7 us (10%)
  other arithmetic  73.7 us (8%)
  Pallas kernels  70.4 us (8%)
  blocking collectives  40 us (4%)
  between operations  15.9 us (2%)
    ppermute x6, waiting for transfers between devices, ring_gather(): from_low = lax.ppermute(blk, 'col', up)  110 us
    ppermute x5, waiting for transfers between devices, ring_scatter(): lax.ppermute(jnp.concatenate([low[:half], low[half:] + from_high], axis=0...  105 us
    dot_general x10, matrix products, dot_tl(): lax.dot_general(lhs, rhs, (((0,), (0,)), ((), ())), preferred_element_typ...  65 us
    dot_general x5, matrix products, dot(): return jnp.dot(lhs, rhs, preferred_element_type=F32)  64.8 us
    pallas_call x2, Pallas kernels, attention_bwd(): pl.pallas_call(functools.partial(attn_bwd_kernel, head_dim ** (-0.5), min...  44.5 us
    dot_general x3, matrix products, dot_tr(): lax.dot_general(lhs, rhs, (((1,), (1,)), ((), ())), preferred_element_typ...  36.1 us
    dynamic_update_slice x28, local copies, waits for them, and re-layouts, place(): return lax.dynamic_update_slice(whole, part, tuple(offs))  30.8 us
    ppermute x5, waiting for transfers between devices, ring_scatter(): lax.ppermute(jnp.concatenate([high[:half] + from_low, high[half:]], axis=...  28.3 us
  transfers between devices with their start and end apart: 61, of which 27 were waited for; matrix products, arithmetic and copies ran while one was open for 32% of the time, Pallas kernels for 8%

profile of v2, /device:TPU:96, one launch (start us, length us, event | category | flops | bytes accessed | tf_op | source)
XLA Modules:
  0.0 888.7 jit_solution(17871384627969506654)
XLA Ops:
  12.4 6.0 collective-permute-start
  18.4 48.8 %collective-permute-done.1 = bf16[2048,384]{1,0:T(8,128)(2,1)S(1)} collective-permute-done((bf16[2048,384]{1,0:T(8,128)(2,1)}, bf16[2048,384]{1,0:T(8,128)(2,1)S(1)}, u32[]{:S(2)}, u32[]{:S(2)}) %collective-permute-start.1) | collective-permute-done | bytes 1572896 | tf_op jit(solution)/shard_map/ppermute | solution.py:199
  79.8 8.1 collective-permute-done.3
  119.2 13.7 %add_convert_fusion.q_ref.k_ref.v_ref = bf16[2048,1536]{1,0:T(8,128)(2,1)} fusion(bf16[1536,1536]{0,1:T(8,128)(2,1)S(1)} %bitcast.72, f32[1536]{0:T(1024)S(1)} %copy-done.29, bf16[2048,1536]{1,0:T(8,128)(2,1)} %constant_dynamic-update-slice_fusion.36, f32[1536]{0:T(1024)S(1)} %copy-done.24, f32[1536]{0:T(1024)S(1)} %get-tuple-element.94, ...), kind=kOutput, calls=%fused_computation.30 | convolution fusion | flops 9688842240 | bytes 17336320 | tf_op jit(solution)/shard_map/dot_general | solution.py:22
  147.3 25.9 %attn_fwd.1 = (bf16[2048,512]{1,0:T(8,128)(2,1)S(1)}, f32[4,1,2048]{2,1,0:T(1,128)S(1)}, f32[4,1,2048]{2,1,0:T(1,128)S(1)}) custom-call(bf16[2048,1536]{1,0:T(8,128)(2,1)} %add_convert_fusion.q_ref.k_ref.v_ref, bf16[2048,1536]{1,0:T(8,128)(2,1)} %add_convert_fusion.q_ref.k_ref.v_ref, bf16[2048,1536]{1,0:T(8,128)(2,1)} %add_convert_fusion.q_ref.k_ref.v_ref), custom_call_target="tpu_custom_call" | custom-call | flops 34359738368 | bytes 9437184 | tf_op jit(solution)/shard_map/attn_fwd/pallas_call | solution.py:112
  173.2 6.0 collective-permute-done.11
  196.3 6.5 collective-permute-done.13
  218.2 5.1 constant_dynamic-update-slice_fusion.13
  232.6 24.7 %collective-permute-done.20 = bf16[512,1536]{1,0:T(8,128)(2,1)S(1)} collective-permute-done((bf16[512,1536]{1,0:T(8,128)(2,1)S(1)}, bf16[512,1536]{1,0:T(8,128)(2,1)S(1)}, u32[]{:S(2)}, u32[]{:S(2)}) %collective-permute-start.20) | collective-permute-done | bytes 1572896 | tf_op jit(solution)/shard_map/ppermute | solution.py:199
  279.7 6.1 copy.35
  287.5 12.0 %convolution_convert_fusion = bf16[2048,1536]{1,0:T(8,128)(2,1)} fusion(bf16[2048,1536]{1,0:T(8,128)(2,1)S(1)} %bitcast.62, bf16[1536,1536]{1,0:T(8,128)(2,1)S(1)} %bitcast.77), kind=kOutput, calls=%fused_computation.33 | convolution fusion | flops 9666822144 | bytes 17301504 | tf_op jit(solution)/shard_map/dot_general | solution.py:26
  304.3 26.2 %fusion.80 = (f32[1536]{0:T(1024)}, bf16[2048,1536]{1,0:T(8,128)(2,1)}, bf16[2048,1536]{1,0:T(8,128)(2,1)}) fusion(f32[1536]{0:T(1024)S(1)} %copy-done.42, bf16[2048,1536]{1,0:T(8,128)(2,1)} %convolution_convert_fusion, bf16[1536,1536]{1,0:T(8,128)(2,1)} %all-gather.11.cloned.1.call-done, bf16[2048,1536]{1,0:T(8,128)(2,1)} %constant_dynamic-update-slice_fusion.9, ...), kind=kOutput, calls=%fused_computation.231 | convolution fusion | flops 9761191936 | bytes 29925376 | tf_op jit(solution)/shard_map/dot_general | solution.py:22
  330.5 12.1 %fusion.46 = f32[2048,1536]{1,0:T(8,128)S(1)} fusion(bf16[1536,1536]{1,0:T(8,128)(2,1)S(1)} %copy-done.41, bf16[2048,1536]{1,0:T(8,128)(2,1)} %get-tuple-element.100), kind=kOutput, calls=%fused_computation.85 | convolution fusion | flops 9663676416 | bytes 23592960 | tf_op jit(solution)/shard_map/dot_general | solution.py:26
  346.5 10.7 %fusion.50 = f32[1536,384]{1,0:T(8,128)} fusion(bf16[2048,1536]{1,0:T(8,128)(2,1)} %get-tuple-element.103, bf16[2048,1536]{1,0:T(8,128)(2,1)} %copy-done.5), kind=kOutput, calls=%fused_computation.95 | convolution fusion | flops 2415919104 | bytes 10223616 | tf_op jit(solution)/shard_map/dot_general | solution.py:30
  388.7 16.1 %fusion.89 = f32[2048,1536]{1,0:T(8,128)} fusion(bf16[2048,1536]{1,0:T(8,128)(2,1)} %get-tuple-element.103, bf16[1536,1536]{1,0:T(8,128)(2,1)} %bitcast.78), kind=kOutput, calls=%fused_computation.238 | convolution fusion | flops 9663676416 | bytes 23592960 | tf_op jit(solution)/shard_map/dot_general | solution.py:22
  404.7 37.5 %collective-permute-done.27 = f32[512,1536]{1,0:T(8,128)} collective-permute-done((f32[512,1536]{1,0:T(8,128)S(1)}, f32[512,1536]{1,0:T(8,128)}, u32[]{:S(2)}, u32[]{:S(2)}) %collective-permute-start.27) | collective-permute-done | bytes 3145760 | tf_op jit(solution)/shard_map/ppermute | solution.py:233
  464.6 30.3 %collective-permute-done.28 = bf16[512,1536]{1,0:T(8,128)(2,1)S(1)} collective-permute-done((bf16[512,1536]{1,0:T(8,128)(2,1)}, bf16[512,1536]{1,0:T(8,128)(2,1)S(1)}, u32[]{:S(2)}, u32[]{:S(2)}) %collective-permute-start.28) | collective-permute-done | bytes 1572896 | tf_op jit(solution)/shard_map/ppermute | solution.py:199
  495.9 14.1 %fusion.44 = f32[1536,1536]{1,0:T(8,128)} fusion(bf16[2048,1536]{1,0:T(8,128)(2,1)S(1)} %bitcast.86, bf16[2048,1536]{1,0:T(8,128)(2,1)} %constant_dynamic-update-slice_fusion.9, f32[1536]{0:T(1024)S(1)} %copy-done.26, f32[1536]{0:T(1024)S(1)} %get-tuple-element.90, f32[2048]{0:T(1024)S(1)} %get-tuple-element.140, f32[2048]{0:T(1024)S(1)} %get-tuple-element.139), kind=kOutput, calls=%fused_computation.83 | convolution fusion | flops 9682550784 | bytes 22048768 | tf_op jit(solution)/shard_map/dot_general | solution.py:30
  518.0 7.3 collective-permute-done.31
  553.3 22.2 %attn_bwd.2.rest_0_ = bf16[2048,1536]{1,0:T(8,128)(2,1)} custom-call(bf16[2048,1536]{1,0:T(8,128)(2,1)} %add_convert_fusion.q_ref.k_ref.v_ref, bf16[2048,1536]{1,0:T(8,128)(2,1)} %add_convert_fusion.q_ref.k_ref.v_ref, bf16[2048,1536]{1,0:T(8,128)(2,1)} %add_convert_fusion.q_ref.k_ref.v_ref, bf16[2048,512]{1,0:T(8,128)(2,1)S(1)} %convolution_convert_fusion.1.do_ref, ...), custom_call_target="tpu_custom_call" | custom-call | flops 42949672960 | bytes 6291456 | tf_op jit(solution)/shard_map/attn_bwd/pallas_call | solution.py:136
  575.5 22.3 %attn_bwd.3 = bf16[2048,1536]{1,0:T(8,128)(2,1)} custom-call(bf16[2048,1536]{1,0:T(8,128)(2,1)} %add_convert_fusion.q_ref.k_ref.v_ref, bf16[2048,1536]{1,0:T(8,128)(2,1)} %add_convert_fusion.q_ref.k_ref.v_ref, bf16[2048,1536]{1,0:T(8,128)(2,1)} %add_convert_fusion.q_ref.k_ref.v_ref, ...), custom_call_target="tpu_custom_call", output_to_operand_aliasing={{}: (6, {})} | custom-call | flops 42949672960 | bytes 6291456 | tf_op jit(solution)/shard_map/attn_bwd/pallas_call | solution.py:136
  597.8 12.0 %fusion.90 = f32[2048,1536]{1,0:T(8,128)S(1)} fusion(bf16[2048,1536]{1,0:T(8,128)(2,1)} %attn_bwd.3, bf16[1536,1536]{0,1:T(8,128)(2,1)S(1)} %bitcast.75), kind=kOutput, calls=%fused_computation.239 | convolution fusion | flops 9663676416 | bytes 23592960 | tf_op jit(solution)/shard_map/dot_general | solution.py:26
  621.7 15.9 %collective-permute-done.42 = f32[1,384]{1,0:T(1,128)S(1)} collective-permute-done((f32[1,384]{1,0:T(1,128)S(1)}, f32[1,384]{1,0:T(1,128)S(1)}, u32[]{:S(2)}, u32[]{:S(2)}) %collective-permute-start.42) | collective-permute-done | bytes 1568 | tf_op jit(solution)/shard_map/ppermute | solution.py:229
  648.2 8.7 copy.36
  656.9 5.3 slice.276
  673.6 26.0 %psum.14 = f32[4224]{0:T(1024)S(1)} all-reduce(f32[4224]{0:T(1024)S(1)} %constant_dynamic-update-slice_fusion.29), channel_id=1, replica_groups=mesh['dp'=1,'col'=4,'row'=8] {'row'}, use_global_device_ids=true, to_apply=%region_18.19 | all-reduce | flops 4224 | bytes 33792 | tf_op jit(solution)/shard_map/psum | solution.py:381
  699.7 15.3 %fusion.77 = f32[1536,1152]{1,0:T(8,128)} fusion(bf16[2048,1152]{0,1:T(8,128)(2,1)} %bitcast.79, bf16[2048,1536]{1,0:T(8,128)(2,1)} %constant_dynamic-update-slice_fusion.36, f32[1536]{0:T(1024)S(1)} %copy-done.25, f32[1536]{0:T(1024)S(1)} %copy-done.23, f32[2048]{0:T(1024)S(1)} %copy-done.33, f32[2048]{0:T(1024)S(1)} %copy-done.31), kind=kOutput, calls=%fused_computation.230 | convolution fusion | flops 7266631680 | bytes 18116608 | tf_op jit(solution)/shard_map/dot_general | solution.py:30
  740.5 65.4 %collective-permute-done.35 = f32[2048,384]{1,0:T(8,128)} collective-permute-done((f32[2048,384]{1,0:T(8,128)}, f32[2048,384]{1,0:T(8,128)}, u32[]{:S(2)}, u32[]{:S(2)}) %collective-permute-start.35) | collective-permute-done | bytes 3145760 | tf_op jit(solution)/shard_map/ppermute | solution.py:233
  805.8 15.9 %collective-permute-done.34 = f32[2048,384]{1,0:T(8,128)} collective-permute-done((f32[2048,384]{1,0:T(8,128)}, f32[2048,384]{1,0:T(8,128)}, u32[]{:S(2)}, u32[]{:S(2)}) %collective-permute-start.34) | collective-permute-done | bytes 3145760 | tf_op jit(solution)/shard_map/ppermute | solution.py:232
  821.7 5.9 fusion.49
  845.8 8.8 collective-permute-done.47
  859.6 13.9 %psum.15 = f32[2,384]{1,0:T(2,128)S(1)} all-reduce(f32[2,384]{1,0:T(2,128)S(1)} %add_add_fusion), channel_id=1, replica_groups=mesh['dp'=1,'col'=4,'row'=8] {'row'}, use_global_device_ids=true, to_apply=%region_23.24 | all-reduce | flops 768 | bytes 6144 | tf_op jit(solution)/shard_map/psum | solution.py:389
  (386 shorter events, 318.0 us)
Async XLA Ops:
  7.2 104.8 %all-gather.5.cloned.1.call-start = ((), (), s32[]{:S(2)}) async-start(), calls=%async_computation.4 | async-start | bytes 3981312 | tf_op jit(solution)/shard_map/all_gather | solution.py:270
  8.0 125.0 %all-gather.7.cloned.1.call-start = ((), (), s32[]{:S(2)}) async-start(), calls=%async_computation.5 | async-start | bytes 1327104 | tf_op jit(solution)/shard_map/all_gather | solution.py:270
  8.1 59.2 %collective-permute-start.1 = (bf16[2048,384]{1,0:T(8,128)(2,1)}, bf16[2048,384]{1,0:T(8,128)(2,1)S(1)}, u32[]{:S(2)}, u32[]{:S(2)}) collective-permute-start(bf16[2048,384]{1,0:T(8,128)(2,1)} %bitcast.81), channel_id=1, source_target_pairs={{0,8},{8,16},{16,24},{24,0},{1,9},{9,17},{17,25},{25,1},{2,10},{10... | collective-permute-start | bytes 4718600 | tf_op jit(solution)/shard_map/ppermute | solution.py:199
  9.7 61.0 %collective-permute-start.2 = (bf16[2048,384]{1,0:T(8,128)(2,1)}, bf16[2048,384]{1,0:T(8,128)(2,1)S(1)}, u32[]{:S(2)}, u32[]{:S(2)}) collective-permute-start(bf16[2048,384]{1,0:T(8,128)(2,1)} %bitcast.82), channel_id=1, source_target_pairs={{0,24},{8,0},{16,8},{24,16},{1,25},{9,1},{17,9},{25,17},{2,26},{10... | collective-permute-start | bytes 4718600 | tf_op jit(solution)/shard_map/ppermute | solution.py:200
  12.4 267.4 %all-gather.9.cloned.1.call-start = ((), (), s32[]{:S(2)}) async-start(), calls=%async_computation.6 | async-start | bytes 5308416 | tf_op jit(solution)/shard_map/all_gather | solution.py:270
  12.4 79.9 %collective-permute-start = (bf16[768,384]{1,0:T(8,128)(2,1)}, bf16[768,384]{1,0:T(8,128)(2,1)}, u32[]{:S(2)}, u32[]{:S(2)}) collective-permute-start(bf16[768,384]{1,0:T(8,128)(2,1)} %param.25), channel_id=1, source_target_pairs={{0,0},{8,2},{16,4},{24,6},{1,1},{9,3},{17,5},{25,7},{2,8},{10,10},... | collective-permute-start | bytes 1769480 | tf_op jit(solution)/shard_map/ppermute | solution.py:305
  92.4 211.8 %all-gather.11.cloned.1.call-start = ((), (), s32[]{:S(2)}) async-start(), calls=%async_computation.7 | async-start | bytes 5308416 | tf_op jit(solution)/shard_map/all_gather | solution.py:270
  103.5 34.5 %collective-permute-start.9 = (bf16[2048,384]{1,0:T(8,128)(2,1)}, bf16[2048,384]{1,0:T(8,128)(2,1)}, u32[]{:S(2)}, u32[]{:S(2)}) collective-permute-start(bf16[2048,384]{1,0:T(8,128)(2,1)} %bitcast), channel_id=1, source_target_pairs={{0,8},{8,16},{16,24},{24,0},{1,9},{9,17},{17,25},{25,1},{2,10},{10... | collective-permute-start | bytes 4718600 | tf_op jit(solution)/shard_map/ppermute | solution.py:199
  103.5 34.5 %collective-permute-start.10 = (bf16[2048,384]{1,0:T(8,128)(2,1)}, bf16[2048,384]{1,0:T(8,128)(2,1)}, u32[]{:S(2)}, u32[]{:S(2)}) collective-permute-start(bf16[2048,384]{1,0:T(8,128)(2,1)} %bitcast), channel_id=1, source_target_pairs={{0,24},{8,0},{16,8},{24,16},{1,25},{9,1},{17,9},{25,17},{2,26},{10... | collective-permute-start | bytes 4718600 | tf_op jit(solution)/shard_map/ppermute | solution.py:200
  138.0 53.7 %collective-permute-start.16 = (bf16[1536,384]{1,0:T(8,128)(2,1)}, bf16[1536,384]{1,0:T(8,128)(2,1)S(1)}, u32[]{:S(2)}, u32[]{:S(2)}) collective-permute-start(bf16[1536,384]{1,0:T(8,128)(2,1)} %all-gather.7.cloned.1.call-done), channel_id=1, source_target_pairs={{0,8},{8,16},{16,24},{24,0},{1,9},{9,17},{17,25},{25,1},{2,10},{10... | collective-permute-start | bytes 3538952 | tf_op jit(solution)/shard_map/ppermute | solution.py:199
  139.3 53.5 %collective-permute-start.17 = (bf16[1536,384]{1,0:T(8,128)(2,1)}, bf16[1536,384]{1,0:T(8,128)(2,1)}, u32[]{:S(2)}, u32[]{:S(2)}) collective-permute-start(bf16[1536,384]{1,0:T(8,128)(2,1)} %all-gather.7.cloned.1.call-done), channel_id=1, source_target_pairs={{0,24},{8,0},{16,8},{24,16},{1,25},{9,1},{17,9},{25,17},{2,26},{10... | collective-permute-start | bytes 3538952 | tf_op jit(solution)/shard_map/ppermute | solution.py:200
  142.4 36.7 %collective-permute-start.11 = (bf16[1024,384]{1,0:T(8,128)(2,1)S(1)}, bf16[1024,384]{1,0:T(8,128)(2,1)}, u32[]{:S(2)}, u32[]{:S(2)}) collective-permute-start(bf16[1024,384]{1,0:T(8,128)(2,1)S(1)} %slice.199), channel_id=1, source_target_pairs={{0,8},{8,16},{16,24},{24,0},{1,9},{9,17},{17,25},{25,1},{2,10},{10... | collective-permute-start | bytes 2359304 | tf_op jit(solution)/shard_map/ppermute | solution.py:203
  143.8 35.4 %collective-permute-start.12 = (bf16[1024,384]{1,0:T(8,128)(2,1)S(1)}, bf16[1024,384]{1,0:T(8,128)(2,1)}, u32[]{:S(2)}, u32[]{:S(2)}) collective-permute-start(bf16[1024,384]{1,0:T(8,128)(2,1)S(1)} %slice.200), channel_id=1, source_target_pairs={{0,24},{8,0},{16,8},{24,16},{1,25},{9,1},{17,9},{25,17},{2,26},{10... | collective-permute-start | bytes 2359304 | tf_op jit(solution)/shard_map/ppermute | solution.py:204
  189.8 351.8 %reduce-scatter.5.cloned.1.call-start = ((), (), s32[]{:S(2)}) async-start(), calls=%async_computation.8 | async-start | bytes 10616832 | tf_op jit(solution)/shard_map/reduce_scatter | solution.py:273
  223.3 34.0 %collective-permute-start.20 = (bf16[512,1536]{1,0:T(8,128)(2,1)S(1)}, bf16[512,1536]{1,0:T(8,128)(2,1)S(1)}, u32[]{:S(2)}, u32[]{:S(2)}) collective-permute-start(bf16[512,1536]{1,0:T(8,128)(2,1)S(1)} %get-tuple-element.160), channel_id=1, source_target_pairs={{0,8},{8,16},{16,24},{24,0},{1,9},{9,17},{17,25},{25,1},{2,10},{10... | collective-permute-start | bytes 4718600 | tf_op jit(solution)/shard_map/ppermute | solution.py:199
  224.8 37.1 %collective-permute-start.21 = (bf16[512,1536]{1,0:T(8,128)(2,1)S(1)}, bf16[512,1536]{1,0:T(8,128)(2,1)}, u32[]{:S(2)}, u32[]{:S(2)}) collective-permute-start(bf16[512,1536]{1,0:T(8,128)(2,1)S(1)} %get-tuple-element.160), channel_id=1, source_target_pairs={{0,24},{8,0},{16,8},{24,16},{1,25},{9,1},{17,9},{25,17},{2,26},{10... | collective-permute-start | bytes 4718600 | tf_op jit(solution)/shard_map/ppermute | solution.py:200
  377.3 64.9 %collective-permute-start.27 = (f32[512,1536]{1,0:T(8,128)S(1)}, f32[512,1536]{1,0:T(8,128)}, u32[]{:S(2)}, u32[]{:S(2)}) collective-permute-start(f32[512,1536]{1,0:T(8,128)S(1)} %pad_maximum_fusion.2), channel_id=1, source_target_pairs={{0,24},{8,0},{16,8},{24,16},{1,25},{9,1},{17,9},{25,17},{2,26},{10... | collective-permute-start | bytes 9437192 | tf_op jit(solution)/shard_map/ppermute | solution.py:233
  383.0 63.5 %collective-permute-start.25 = (f32[512,1536]{1,0:T(8,128)}, f32[512,1536]{1,0:T(8,128)}, u32[]{:S(2)}, u32[]{:S(2)}) collective-permute-start(f32[512,1536]{1,0:T(8,128)} %pad_maximum_fusion.1), channel_id=1, source_target_pairs={{0,8},{8,16},{16,24},{24,0},{1,9},{9,17},{17,25},{25,1},{2,10},{10... | collective-permute-start | bytes 9437192 | tf_op jit(solution)/shard_map/ppermute | solution.py:232
  451.1 272.7 %reduce-scatter.7.cloned.1.call-start = ((), (), s32[]{:S(2)}) async-start(), calls=%async_computation.9 | async-start | bytes 10616832 | tf_op jit(solution)/shard_map/reduce_scatter | solution.py:273
  461.4 48.6 %collective-permute-start.29 = (bf16[512,1536]{1,0:T(8,128)(2,1)}, bf16[512,1536]{1,0:T(8,128)(2,1)S(1)}, u32[]{:S(2)}, u32[]{:S(2)}) collective-permute-start(bf16[512,1536]{1,0:T(8,128)(2,1)} %get-tuple-element.102), channel_id=1, source_target_pairs={{0,24},{8,0},{16,8},{24,16},{1,25},{9,1},{17,9},{25,17},{2,26},{10... | collective-permute-start | bytes 4718600 | tf_op jit(solution)/shard_map/ppermute | solution.py:200
  526.3 301.4 %reduce-scatter.11.cloned.1.call-start = ((), (), s32[]{:S(2)}) async-start(), calls=%async_computation.11 | async-start | bytes 2654208 | tf_op jit(solution)/shard_map/reduce_scatter | solution.py:273
  534.2 41.4 %collective-permute-start.32 = (f32[1024,384]{1,0:T(8,128)}, f32[1024,384]{1,0:T(8,128)}, u32[]{:S(2)}, u32[]{:S(2)}) collective-permute-start(f32[1024,384]{1,0:T(8,128)} %get-tuple-element.115), channel_id=1, source_target_pairs={{0,8},{8,16},{16,24},{24,0},{1,9},{9,17},{17,25},{25,1},{2,10},{10... | collective-permute-start | bytes 4718600 | tf_op jit(solution)/shard_map/ppermute | solution.py:228
  534.2 41.4 %collective-permute-start.33 = (f32[1024,384]{1,0:T(8,128)}, f32[1024,384]{1,0:T(8,128)}, u32[]{:S(2)}, u32[]{:S(2)}) collective-permute-start(f32[1024,384]{1,0:T(8,128)} %get-tuple-element.114), channel_id=1, source_target_pairs={{0,24},{8,0},{16,8},{24,16},{1,25},{9,1},{17,9},{25,17},{2,26},{10... | collective-permute-start | bytes 4718600 | tf_op jit(solution)/shard_map/ppermute | solution.py:229
  616.2 46.1 %collective-permute-start.36 = (f32[256,1536]{1,0:T(8,128)}, f32[256,1536]{1,0:T(8,128)S(1)}, u32[]{:S(2)}, u32[]{:S(2)}) collective-permute-start(f32[256,1536]{1,0:T(8,128)} %get-tuple-element.108), channel_id=1, source_target_pairs={{0,8},{8,16},{16,24},{24,0},{1,9},{9,17},{17,25},{25,1},{2,10},{10... | collective-permute-start | bytes 4718600 | tf_op jit(solution)/shard_map/ppermute | solution.py:228
  616.2 46.1 %collective-permute-start.38 = (f32[256,1536]{1,0:T(8,128)}, f32[256,1536]{1,0:T(8,128)S(1)}, u32[]{:S(2)}, u32[]{:S(2)}) collective-permute-start(f32[256,1536]{1,0:T(8,128)} %get-tuple-element.109), channel_id=1, source_target_pairs={{0,24},{8,0},{16,8},{24,16},{1,25},{9,1},{17,9},{25,17},{2,26},{10... | collective-permute-start | bytes 4718600 | tf_op jit(solution)/shard_map/ppermute | solution.py:229
  662.2 213.1 %reduce-scatter.9.cloned.1.call-start = ((), (), s32[]{:S(2)}) async-start(), calls=%async_computation.10 | async-start | bytes 7962624 | tf_op jit(solution)/shard_map/reduce_scatter | solution.py:273
  666.4 49.7 %collective-permute-start.39 = (f32[512,1536]{1,0:T(8,128)S(1)}, f32[512,1536]{1,0:T(8,128)}, u32[]{:S(2)}, u32[]{:S(2)}) collective-permute-start(f32[512,1536]{1,0:T(8,128)S(1)} %pad_maximum_fusion.6), channel_id=1, source_target_pairs={{0,24},{8,0},{16,8},{24,16},{1,25},{9,1},{17,9},{25,17},{2,26},{10... | collective-permute-start | bytes 9437192 | tf_op jit(solution)/shard_map/ppermute | solution.py:233
  668.4 50.9 %collective-permute-start.37 = (f32[512,1536]{1,0:T(8,128)}, f32[512,1536]{1,0:T(8,128)}, u32[]{:S(2)}, u32[]{:S(2)}) collective-permute-start(f32[512,1536]{1,0:T(8,128)} %pad_maximum_fusion.5), channel_id=1, source_target_pairs={{0,8},{8,16},{16,24},{24,0},{1,9},{9,17},{17,25},{25,1},{2,10},{10... | collective-permute-start | bytes 9437192 | tf_op jit(solution)/shard_map/ppermute | solution.py:232
  730.0 75.8 %collective-permute-start.35 = (f32[2048,384]{1,0:T(8,128)}, f32[2048,384]{1,0:T(8,128)}, u32[]{:S(2)}, u32[]{:S(2)}) collective-permute-start(f32[2048,384]{1,0:T(8,128)} %pad_maximum_fusion.4), channel_id=1, source_target_pairs={{0,24},{8,0},{16,8},{24,16},{1,25},{9,1},{17,9},{25,17},{2,26},{10... | collective-permute-start | bytes 9437192 | tf_op jit(solution)/shard_map/ppermute | solution.py:233
  731.9 89.8 %collective-permute-start.34 = (f32[2048,384]{1,0:T(8,128)}, f32[2048,384]{1,0:T(8,128)}, u32[]{:S(2)}, u32[]{:S(2)}) collective-permute-start(f32[2048,384]{1,0:T(8,128)} %pad_maximum_fusion.3), channel_id=1, source_target_pairs={{0,8},{8,16},{16,24},{24,0},{1,9},{9,17},{17,25},{25,1},{2,10},{10... | collective-permute-start | bytes 9437192 | tf_op jit(solution)/shard_map/ppermute | solution.py:232
  829.3 44.8 %collective-permute-start.51 = (bf16[192,384]{1,0:T(8,128)(2,1)}, bf16[192,384]{1,0:T(8,128)(2,1)}, u32[]{:S(2)}, u32[]{:S(2)}) collective-permute-start(bf16[192,384]{1,0:T(8,128)(2,1)} %convert_element_type.125), channel_id=1, source_target_pairs={{0,0},{8,2},{16,4},{24,6},{1,1},{9,3},{17,5},{25,7},{2,8},{10,10},... | collective-permute-start | bytes 442376 | tf_op jit(solution)/shard_map/ppermute | solution.py:287
  838.6 35.5 %collective-permute-start.44 = (bf16[512,384]{1,0:T(8,128)(2,1)S(1)}, bf16[512,384]{1,0:T(8,128)(2,1)S(1)}, u32[]{:S(2)}, u32[]{:S(2)}) collective-permute-start(bf16[512,384]{1,0:T(8,128)(2,1)S(1)} %get-tuple-element.124), channel_id=1, source_target_pairs={{0,8},{8,16},{16,24},{24,0},{1,9},{9,17},{17,25},{25,1},{2,10},{10... | collective-permute-start | bytes 1179656 | tf_op jit(solution)/shard_map/ppermute | solution.py:249
  (84 other events, 1194.9 us)
Sparse Core Ops, SparseCore 0:
  9.6 49.6 all-gather.4
  60.9 20.0 all-gather.6
  92.5 33.5 all-gather.8
  189.9 33.2 all-gather.10
  451.2 58.2 reduce-scatter.4
  526.4 59.5 reduce-scatter.6
  662.4 36.0 reduce-scatter.10
  724.0 70.3 reduce-scatter.8
